TPU v7x, 32 devices: a whole 2x2x4 slice. The times are simulated.
32 devices in a mesh: gx: 4 (over x, core), gy: 2 (over y), gz: 4 (over z).
Axes of the slice: x: 2, y: 2, z: 4, core: 2. Of those that a mesh axis runs over, the one named last changes fastest.
Arguments:
- positions: float32 [3, 4, 2, 4, 256], P(None, 'gx', 'gy', 'gz'), may hold values from 0 to 4, as said below
- velocities: float32 [3, 4, 2, 4, 256], P(None, 'gx', 'gy', 'gz'), may hold values from -6 to 6
- forces: float32 [3, 4, 2, 4, 256], P(None, 'gx', 'gy', 'gz'), may hold values from -6 to 6
- charges: float32 [4, 2, 4, 256], P('gx', 'gy', 'gz'), may hold values from -2 to 2
- inverse_mass: float32 [4, 2, 4, 256], P('gx', 'gy', 'gz'), may hold values from 0.5 to 2
- occupancy: int32 [4, 2, 4], P('gx', 'gy', 'gz'), may hold values from 128 to 256
- molecule: int32 [4, 2, 4, 256], P('gx', 'gy', 'gz'), may hold values from 0 to 127, never falling along the last dimension, each value on 1 to 4 neighbouring positions
Outputs:
- positions_out: float32 [3, 4, 2, 4, 256], P(None, 'gx', 'gy', 'gz')
- velocities_out: float32 [3, 4, 2, 4, 256], P(None, 'gx', 'gy', 'gz')
- forces_out: float32 [3, 4, 2, 4, 256], P(None, 'gx', 'gy', 'gz')
Inputs may be any that keep to these rules, and one draw needn't show every extreme that they name: `positions`: component c of a particle of the box with index k along dimension c lies in [k, k + 1).
All inputs are finite; a program needn't handle non-finite values.
Results may differ from a plain program's by a relative error of at most 0.0003.
Values sent between devices are 32-bit elements; how exact they have to be, the bound alone decides.
No kernel may reach another device: no remote copies, remote signals or barrier semaphores. Data moves between devices by JAX's collectives and lax.ppermute only.
A program may use at most 64 MiB of HBM per device.

v0:
```python
import jax
import jax.numpy as jnp
from jax import lax
from jax.sharding import PartitionSpec as P

cutoff_square = 4.0
soften_square = 0.25
time_step = 0.1
half_step = 0.05


def passed_along(block, axis, distance):
    devices = range(lax.axis_size(axis))
    route = [((i - distance) % len(devices), i) for i in devices]
    return lax.ppermute(block, axis, route)


def separations_of(target_places, source_places, lengths):
    separations = []
    for component in range(3):
        spacing = target_places[component][:, None] - source_places[component][None, :]
        separations.append(
            spacing - lengths[component] * jnp.floor(spacing / lengths[component] + 0.5)
        )
    squared = (
        separations[0] * separations[0]
        + separations[1] * separations[1]
        + separations[2] * separations[2]
    )
    switch = jnp.maximum(1.0 - squared / cutoff_square, 0.0)
    soften = squared + soften_square
    return (separations, switch * switch / (soften * jnp.sqrt(soften)))


def interact(target_places, target_charge, source_places, source_charge, lengths, pair_mask):
    separations, base = separations_of(target_places, source_places, lengths)
    weight = source_charge[None, :] * base
    if pair_mask is not None:
        weight = weight * pair_mask
    return jnp.stack(
        [target_charge * jnp.sum(weight * separation, axis=-1) for separation in separations]
    )


def cycle_offsets(cycle_size):
    if cycle_size >= 5:
        return [1, -1, 2, -2]
    return list(range(1, cycle_size))


def across_second(gathered):
    pieces = [gathered]
    for offset in cycle_offsets(lax.axis_size("gy")):
        pieces.append(passed_along(gathered, "gy", offset))
    return jnp.stack(pieces)


def across_first(gathered):
    pieces = [gathered]
    for offset in cycle_offsets(lax.axis_size("gx")):
        pieces.append(passed_along(gathered, "gx", offset))
    return jnp.stack(pieces)


def forward_sum(summed, places, charge_live, blocks, lengths):

    def advance(total, column):
        return (total + interact(places, charge_live, column[:3], column[3], lengths, None), None)

    result, unused = lax.scan(advance, summed, blocks)
    return result


def full_shell(places, charge_live, tower_data, lengths):
    stacked = across_first(across_second(tower_data))
    blocks = stacked.reshape(-1, 4, tower_data.shape[1])
    return forward_sum(jnp.zeros_like(places), places, charge_live, blocks, lengths)


def force_field(places, charge_live, same_molecule, lengths):
    sources = jnp.concatenate([places, charge_live[None]], axis=0)
    tower_data = lax.all_gather(sources, "gz", axis=1, tiled=True)
    summed = full_shell(places, charge_live, tower_data, lengths)
    return summed - interact(places, charge_live, places, charge_live, lengths, same_molecule)


def local(positions, velocities, forces, charges, inverse_mass, occupancy, molecule):
    lengths = (float(lax.axis_size("gx")), float(lax.axis_size("gy")), float(lax.axis_size("gz")))
    shape = positions.shape
    places = positions.reshape(3, -1)
    velocity = velocities.reshape(3, -1)
    current = forces.reshape(3, -1)
    slots_count = places.shape[1]
    slots = jnp.arange(slots_count, dtype=jnp.int32)
    charge_live = jnp.where(slots < occupancy.reshape(()), charges.reshape(-1), jnp.float32(0.0))
    mass_inverse = inverse_mass.reshape(-1)
    labels = molecule.reshape(-1)
    same_molecule = (labels[:, None] == labels[None, :]).astype(jnp.float32)
    for turn in range(2):
        midway = velocity + half_step * mass_inverse * current
        places = places + time_step * midway
        current = force_field(places, charge_live, same_molecule, lengths)
        velocity = midway + half_step * mass_inverse * current
    return (places.reshape(shape), velocity.reshape(shape), current.reshape(shape))


def solution(mesh):
    in_specs = (
        P(None, "gx", "gy", "gz", None),
        P(None, "gx", "gy", "gz", None),
        P(None, "gx", "gy", "gz", None),
        P("gx", "gy", "gz", None),
        P("gx", "gy", "gz", None),
        P("gx", "gy", "gz"),
        P("gx", "gy", "gz", None),
    )
    out_specs = (
        P(None, "gx", "gy", "gz", None),
        P(None, "gx", "gy", "gz", None),
        P(None, "gx", "gy", "gz", None),
    )
    return jax.shard_map(local, mesh=mesh, in_specs=in_specs, out_specs=out_specs, check_vma=False)
```

profile of v0, /device:TPU:0, one launch (start us, length us, event | category | flops | bytes accessed | tf_op | source)
XLA Modules:
  0.0 83.9 jit_solution(9478626252136731197)
XLA Ops:
  4.7 14.9 %all_gather.6 = f32[4,1024]{1,0:T(4,128)S(1)} all-gather(f32[4,256]{1,0:T(4,128)S(1)} %pad_maximum_fusion.5), channel_id=1, replica_groups=mesh['gx'=4,'gy'=2,'gz'=4] {'gz'}, dimensions={1}, use_global_device_ids=true | all-gather | bytes 20480 | tf_op jit(solution)/shard_map/all_gather | solution.py:82
  19.7 1.5 %collective-permute-start = (f32[4,1024]{1,0:T(4,128)S(1)}, f32[4,1024]{1,0:T(4,128)S(1)}, u32[]{:S(2)}, u32[]{:S(2)}) collective-permute-start(f32[4,1024]{1,0:T(4,128)S(1)} %all_gather.6), channel_id=1, source_target_pairs={{4,0},{0,4},{5,1},{1,5},{6,2},{2,6},{7,3},{3,7},{12,8},{8,12},{13,... | collective-permute-start | bytes 49160 | tf_op jit(solution)/shard_map/ppermute | solution.py:15
  21.2 2.2 %collective-permute-done = f32[4,1024]{1,0:T(4,128)S(1)} collective-permute-done((f32[4,1024]{1,0:T(4,128)S(1)}, f32[4,1024]{1,0:T(4,128)S(1)}, u32[]{:S(2)}, u32[]{:S(2)}) %collective-permute-start) | collective-permute-done | bytes 16416 | tf_op jit(solution)/shard_map/ppermute | solution.py:15
  23.5 1.6 %collective-permute-start.2 = (f32[2,4,1024]{2,1,0:T(4,128)S(1)}, f32[2,4,1024]{2,1,0:T(4,128)S(1)}, u32[]{:S(2)}, u32[]{:S(2)}) collective-permute-start(f32[2,4,1024]{2,1,0:T(4,128)S(1)} %get-tuple-element.156), channel_id=1, source_target_pairs={{16,0},{24,8},{0,16},{8,24},{17,1},{25,9},{1,17},{9,25},{18,2},{26... | collective-permute-start | bytes 98312 | tf_op jit(solution)/shard_map/ppermute | solution.py:15
  28.1 16.3 %while.22 = (s32[]{:T(128)}, f32[3,256]{1,0:T(4,128)S(1)}, f32[8,4,1024]{2,1,0:T(4,128)S(1)}, f32[3,256]{1,0:T(4,128)S(1)}, f32[256]{0:T(256)S(1)}, /*index=5*/s32[]{:T(128)}, s32[]{:T(128)}, s32[]{}, s32[]{}, s32[]{}) while((s32[]{:T(128)}, f32[3,256]{1,0:T(4,128)S(1)}, f32[8,4,1024]{2,1,0:T(4,128)S(1)}, f32[3,256]{1,0:T(4,128)S(1)}, ...), condition=%wide.region_4.5_spmd.clone, body=%wide.region_0.4_spmd.clone.sunk | while | flops 9702406 | bytes 77987 | solution.py:70
  28.1 1.9 %fusion.108 = (f32[256]{0:T(256)S(1)}, f32[256]{0:T(256)S(1)}, f32[256]{0:T(256)S(1)}) fusion(f32[1024]{0:T(1024)S(1)} %bitcast.119, f32[256]{0:T(256)S(1)} %bitcast.141, f32[1024]{0:T(1024)S(1)} %bitcast.120, f32[256]{0:T(256)S(1)} %bitcast.140, f32[1024]{0:T(1024)S(1)} %bitcast.118, f32[256]{0:T(256)S(1)} %bitcast.139, f32[1024]{0:T(1024)S(1)} %bitcast.117), kind=kLoop, calls=%fused_computation.14.clone.1 | loop fusion | flops 9698560 | bytes 22528 | tf_op jit(solution)/shard_map/while/body/eval_jaxpr/reduce_sum | solution.py:41
  30.1 1.9 %fusion.108 = (f32[256]{0:T(256)S(1)}, f32[256]{0:T(256)S(1)}, f32[256]{0:T(256)S(1)}) fusion(f32[1024]{0:T(1024)S(1)} %bitcast.119, f32[256]{0:T(256)S(1)} %bitcast.141, f32[1024]{0:T(1024)S(1)} %bitcast.120, f32[256]{0:T(256)S(1)} %bitcast.140, f32[1024]{0:T(1024)S(1)} %bitcast.118, f32[256]{0:T(256)S(1)} %bitcast.139, f32[1024]{0:T(1024)S(1)} %bitcast.117), kind=kLoop, calls=%fused_computation.14.clone.1 | loop fusion | flops 9698560 | bytes 22528 | tf_op jit(solution)/shard_map/while/body/eval_jaxpr/reduce_sum | solution.py:41
  32.2 1.9 %fusion.108 = (f32[256]{0:T(256)S(1)}, f32[256]{0:T(256)S(1)}, f32[256]{0:T(256)S(1)}) fusion(f32[1024]{0:T(1024)S(1)} %bitcast.119, f32[256]{0:T(256)S(1)} %bitcast.141, f32[1024]{0:T(1024)S(1)} %bitcast.120, f32[256]{0:T(256)S(1)} %bitcast.140, f32[1024]{0:T(1024)S(1)} %bitcast.118, f32[256]{0:T(256)S(1)} %bitcast.139, f32[1024]{0:T(1024)S(1)} %bitcast.117), kind=kLoop, calls=%fused_computation.14.clone.1 | loop fusion | flops 9698560 | bytes 22528 | tf_op jit(solution)/shard_map/while/body/eval_jaxpr/reduce_sum | solution.py:41
  34.2 1.9 %fusion.108 = (f32[256]{0:T(256)S(1)}, f32[256]{0:T(256)S(1)}, f32[256]{0:T(256)S(1)}) fusion(f32[1024]{0:T(1024)S(1)} %bitcast.119, f32[256]{0:T(256)S(1)} %bitcast.141, f32[1024]{0:T(1024)S(1)} %bitcast.120, f32[256]{0:T(256)S(1)} %bitcast.140, f32[1024]{0:T(1024)S(1)} %bitcast.118, f32[256]{0:T(256)S(1)} %bitcast.139, f32[1024]{0:T(1024)S(1)} %bitcast.117), kind=kLoop, calls=%fused_computation.14.clone.1 | loop fusion | flops 9698560 | bytes 22528 | tf_op jit(solution)/shard_map/while/body/eval_jaxpr/reduce_sum | solution.py:41
  36.2 1.9 %fusion.108 = (f32[256]{0:T(256)S(1)}, f32[256]{0:T(256)S(1)}, f32[256]{0:T(256)S(1)}) fusion(f32[1024]{0:T(1024)S(1)} %bitcast.119, f32[256]{0:T(256)S(1)} %bitcast.141, f32[1024]{0:T(1024)S(1)} %bitcast.120, f32[256]{0:T(256)S(1)} %bitcast.140, f32[1024]{0:T(1024)S(1)} %bitcast.118, f32[256]{0:T(256)S(1)} %bitcast.139, f32[1024]{0:T(1024)S(1)} %bitcast.117), kind=kLoop, calls=%fused_computation.14.clone.1 | loop fusion | flops 9698560 | bytes 22528 | tf_op jit(solution)/shard_map/while/body/eval_jaxpr/reduce_sum | solution.py:41
  38.3 1.9 %fusion.108 = (f32[256]{0:T(256)S(1)}, f32[256]{0:T(256)S(1)}, f32[256]{0:T(256)S(1)}) fusion(f32[1024]{0:T(1024)S(1)} %bitcast.119, f32[256]{0:T(256)S(1)} %bitcast.141, f32[1024]{0:T(1024)S(1)} %bitcast.120, f32[256]{0:T(256)S(1)} %bitcast.140, f32[1024]{0:T(1024)S(1)} %bitcast.118, f32[256]{0:T(256)S(1)} %bitcast.139, f32[1024]{0:T(1024)S(1)} %bitcast.117), kind=kLoop, calls=%fused_computation.14.clone.1 | loop fusion | flops 9698560 | bytes 22528 | tf_op jit(solution)/shard_map/while/body/eval_jaxpr/reduce_sum | solution.py:41
  40.3 1.9 %fusion.108 = (f32[256]{0:T(256)S(1)}, f32[256]{0:T(256)S(1)}, f32[256]{0:T(256)S(1)}) fusion(f32[1024]{0:T(1024)S(1)} %bitcast.119, f32[256]{0:T(256)S(1)} %bitcast.141, f32[1024]{0:T(1024)S(1)} %bitcast.120, f32[256]{0:T(256)S(1)} %bitcast.140, f32[1024]{0:T(1024)S(1)} %bitcast.118, f32[256]{0:T(256)S(1)} %bitcast.139, f32[1024]{0:T(1024)S(1)} %bitcast.117), kind=kLoop, calls=%fused_computation.14.clone.1 | loop fusion | flops 9698560 | bytes 22528 | tf_op jit(solution)/shard_map/while/body/eval_jaxpr/reduce_sum | solution.py:41
  42.3 1.9 %fusion.108 = (f32[256]{0:T(256)S(1)}, f32[256]{0:T(256)S(1)}, f32[256]{0:T(256)S(1)}) fusion(f32[1024]{0:T(1024)S(1)} %bitcast.119, f32[256]{0:T(256)S(1)} %bitcast.141, f32[1024]{0:T(1024)S(1)} %bitcast.120, f32[256]{0:T(256)S(1)} %bitcast.140, f32[1024]{0:T(1024)S(1)} %bitcast.118, f32[256]{0:T(256)S(1)} %bitcast.139, f32[1024]{0:T(1024)S(1)} %bitcast.117), kind=kLoop, calls=%fused_computation.14.clone.1 | loop fusion | flops 9698560 | bytes 22528 | tf_op jit(solution)/shard_map/while/body/eval_jaxpr/reduce_sum | solution.py:41
  45.1 13.2 %all_gather.7 = f32[4,1024]{1,0:T(4,128)S(1)} all-gather(f32[4,256]{1,0:T(4,128)S(1)} %pad_maximum_fusion.4), channel_id=1, replica_groups=mesh['gx'=4,'gy'=2,'gz'=4] {'gz'}, dimensions={1}, use_global_device_ids=true | all-gather | bytes 20480 | tf_op jit(solution)/shard_map/all_gather | solution.py:82
  60.4 1.6 %collective-permute-done.4 = f32[4,1024]{1,0:T(4,128)S(1)} collective-permute-done((f32[4,1024]{1,0:T(4,128)S(1)}, f32[4,1024]{1,0:T(4,128)S(1)}, u32[]{:S(2)}, u32[]{:S(2)}) %collective-permute-start.4) | collective-permute-done | bytes 16416 | tf_op jit(solution)/shard_map/ppermute | solution.py:15
  66.4 16.3 %while.23 = (s32[]{:T(128)}, f32[3,256]{1,0:T(4,128)S(1)}, f32[8,4,1024]{2,1,0:T(4,128)S(1)}, f32[3,256]{1,0:T(4,128)S(1)}, f32[256]{0:T(256)S(1)}, /*index=5*/s32[]{:T(128)}, s32[]{:T(128)}, s32[]{}, s32[]{}, s32[]{}) while((s32[]{:T(128)}, f32[3,256]{1,0:T(4,128)S(1)}, f32[8,4,1024]{2,1,0:T(4,128)S(1)}, ...), condition=%wide.region_12.13_spmd.clone, body=%wide.region_8.12_spmd.clone.sunk | while | flops 9702406 | bytes 77987 | solution.py:70
  66.5 1.9 %fusion.111 = (f32[256]{0:T(256)S(1)}, f32[256]{0:T(256)S(1)}, f32[256]{0:T(256)S(1)}) fusion(f32[1024]{0:T(1024)S(1)} %bitcast.123, f32[256]{0:T(256)S(1)} %bitcast.144, f32[1024]{0:T(1024)S(1)} %bitcast.124, f32[256]{0:T(256)S(1)} %bitcast.143, f32[1024]{0:T(1024)S(1)} %bitcast.122, f32[256]{0:T(256)S(1)} %bitcast.142, f32[1024]{0:T(1024)S(1)} %bitcast.121), kind=kLoop, calls=%fused_computation.48.clone.1 | loop fusion | flops 9698560 | bytes 22528 | tf_op jit(solution)/shard_map/while/body/eval_jaxpr/reduce_sum | solution.py:41
  68.5 1.9 %fusion.111 = (f32[256]{0:T(256)S(1)}, f32[256]{0:T(256)S(1)}, f32[256]{0:T(256)S(1)}) fusion(f32[1024]{0:T(1024)S(1)} %bitcast.123, f32[256]{0:T(256)S(1)} %bitcast.144, f32[1024]{0:T(1024)S(1)} %bitcast.124, f32[256]{0:T(256)S(1)} %bitcast.143, f32[1024]{0:T(1024)S(1)} %bitcast.122, f32[256]{0:T(256)S(1)} %bitcast.142, f32[1024]{0:T(1024)S(1)} %bitcast.121), kind=kLoop, calls=%fused_computation.48.clone.1 | loop fusion | flops 9698560 | bytes 22528 | tf_op jit(solution)/shard_map/while/body/eval_jaxpr/reduce_sum | solution.py:41
  70.5 1.9 %fusion.111 = (f32[256]{0:T(256)S(1)}, f32[256]{0:T(256)S(1)}, f32[256]{0:T(256)S(1)}) fusion(f32[1024]{0:T(1024)S(1)} %bitcast.123, f32[256]{0:T(256)S(1)} %bitcast.144, f32[1024]{0:T(1024)S(1)} %bitcast.124, f32[256]{0:T(256)S(1)} %bitcast.143, f32[1024]{0:T(1024)S(1)} %bitcast.122, f32[256]{0:T(256)S(1)} %bitcast.142, f32[1024]{0:T(1024)S(1)} %bitcast.121), kind=kLoop, calls=%fused_computation.48.clone.1 | loop fusion | flops 9698560 | bytes 22528 | tf_op jit(solution)/shard_map/while/body/eval_jaxpr/reduce_sum | solution.py:41
  72.6 1.9 %fusion.111 = (f32[256]{0:T(256)S(1)}, f32[256]{0:T(256)S(1)}, f32[256]{0:T(256)S(1)}) fusion(f32[1024]{0:T(1024)S(1)} %bitcast.123, f32[256]{0:T(256)S(1)} %bitcast.144, f32[1024]{0:T(1024)S(1)} %bitcast.124, f32[256]{0:T(256)S(1)} %bitcast.143, f32[1024]{0:T(1024)S(1)} %bitcast.122, f32[256]{0:T(256)S(1)} %bitcast.142, f32[1024]{0:T(1024)S(1)} %bitcast.121), kind=kLoop, calls=%fused_computation.48.clone.1 | loop fusion | flops 9698560 | bytes 22528 | tf_op jit(solution)/shard_map/while/body/eval_jaxpr/reduce_sum | solution.py:41
  74.6 1.9 %fusion.111 = (f32[256]{0:T(256)S(1)}, f32[256]{0:T(256)S(1)}, f32[256]{0:T(256)S(1)}) fusion(f32[1024]{0:T(1024)S(1)} %bitcast.123, f32[256]{0:T(256)S(1)} %bitcast.144, f32[1024]{0:T(1024)S(1)} %bitcast.124, f32[256]{0:T(256)S(1)} %bitcast.143, f32[1024]{0:T(1024)S(1)} %bitcast.122, f32[256]{0:T(256)S(1)} %bitcast.142, f32[1024]{0:T(1024)S(1)} %bitcast.121), kind=kLoop, calls=%fused_computation.48.clone.1 | loop fusion | flops 9698560 | bytes 22528 | tf_op jit(solution)/shard_map/while/body/eval_jaxpr/reduce_sum | solution.py:41
  76.6 1.9 %fusion.111 = (f32[256]{0:T(256)S(1)}, f32[256]{0:T(256)S(1)}, f32[256]{0:T(256)S(1)}) fusion(f32[1024]{0:T(1024)S(1)} %bitcast.123, f32[256]{0:T(256)S(1)} %bitcast.144, f32[1024]{0:T(1024)S(1)} %bitcast.124, f32[256]{0:T(256)S(1)} %bitcast.143, f32[1024]{0:T(1024)S(1)} %bitcast.122, f32[256]{0:T(256)S(1)} %bitcast.142, f32[1024]{0:T(1024)S(1)} %bitcast.121), kind=kLoop, calls=%fused_computation.48.clone.1 | loop fusion | flops 9698560 | bytes 22528 | tf_op jit(solution)/shard_map/while/body/eval_jaxpr/reduce_sum | solution.py:41
  78.7 1.9 %fusion.111 = (f32[256]{0:T(256)S(1)}, f32[256]{0:T(256)S(1)}, f32[256]{0:T(256)S(1)}) fusion(f32[1024]{0:T(1024)S(1)} %bitcast.123, f32[256]{0:T(256)S(1)} %bitcast.144, f32[1024]{0:T(1024)S(1)} %bitcast.124, f32[256]{0:T(256)S(1)} %bitcast.143, f32[1024]{0:T(1024)S(1)} %bitcast.122, f32[256]{0:T(256)S(1)} %bitcast.142, f32[1024]{0:T(1024)S(1)} %bitcast.121), kind=kLoop, calls=%fused_computation.48.clone.1 | loop fusion | flops 9698560 | bytes 22528 | tf_op jit(solution)/shard_map/while/body/eval_jaxpr/reduce_sum | solution.py:41
  80.7 1.9 %fusion.111 = (f32[256]{0:T(256)S(1)}, f32[256]{0:T(256)S(1)}, f32[256]{0:T(256)S(1)}) fusion(f32[1024]{0:T(1024)S(1)} %bitcast.123, f32[256]{0:T(256)S(1)} %bitcast.144, f32[1024]{0:T(1024)S(1)} %bitcast.124, f32[256]{0:T(256)S(1)} %bitcast.143, f32[1024]{0:T(1024)S(1)} %bitcast.122, f32[256]{0:T(256)S(1)} %bitcast.142, f32[1024]{0:T(1024)S(1)} %bitcast.121), kind=kLoop, calls=%fused_computation.48.clone.1 | loop fusion | flops 9698560 | bytes 22528 | tf_op jit(solution)/shard_map/while/body/eval_jaxpr/reduce_sum | solution.py:41
  (107 shorter events, 15.9 us)
Async XLA Ops:
  0.6 0.7 copy-start
  2.7 0.7 copy-start.2
  3.4 0.7 copy-start.3
  19.7 3.7 %collective-permute-start = (f32[4,1024]{1,0:T(4,128)S(1)}, f32[4,1024]{1,0:T(4,128)S(1)}, u32[]{:S(2)}, u32[]{:S(2)}) collective-permute-start(f32[4,1024]{1,0:T(4,128)S(1)} %all_gather.6), channel_id=1, source_target_pairs={{4,0},{0,4},{5,1},{1,5},{6,2},{2,6},{7,3},{3,7},{12,8},{8,12},{13,... | collective-permute-start | bytes 49160 | tf_op jit(solution)/shard_map/ppermute | solution.py:15
  23.4 3.4 %collective-permute-start.1 = (f32[2,4,1024]{2,1,0:T(4,128)S(1)}, f32[2,4,1024]{2,1,0:T(4,128)S(1)}, u32[]{:S(2)}, u32[]{:S(2)}) collective-permute-start(f32[2,4,1024]{2,1,0:T(4,128)S(1)} %get-tuple-element.156), channel_id=1, source_target_pairs={{24,0},{0,8},{8,16},{16,24},{25,1},{1,9},{9,17},{17,25},{26,2},{2,... | collective-permute-start | bytes 98312 | tf_op jit(solution)/shard_map/ppermute | solution.py:15
  23.5 4.0 %collective-permute-start.2 = (f32[2,4,1024]{2,1,0:T(4,128)S(1)}, f32[2,4,1024]{2,1,0:T(4,128)S(1)}, u32[]{:S(2)}, u32[]{:S(2)}) collective-permute-start(f32[2,4,1024]{2,1,0:T(4,128)S(1)} %get-tuple-element.156), channel_id=1, source_target_pairs={{16,0},{24,8},{0,16},{8,24},{17,1},{25,9},{1,17},{9,25},{18,2},{26... | collective-permute-start | bytes 98312 | tf_op jit(solution)/shard_map/ppermute | solution.py:15
  25.0 3.0 %collective-permute-start.3 = (f32[2,4,1024]{2,1,0:T(4,128)S(1)}, f32[2,4,1024]{2,1,0:T(4,128)S(1)}, u32[]{:S(2)}, u32[]{:S(2)}) collective-permute-start(f32[2,4,1024]{2,1,0:T(4,128)S(1)} %get-tuple-element.156), channel_id=1, source_target_pairs={{8,0},{16,8},{24,16},{0,24},{9,1},{17,9},{25,17},{1,25},{10,2},{18... | collective-permute-start | bytes 98312 | tf_op jit(solution)/shard_map/ppermute | solution.py:15
  44.3 0.7 copy-start.1
  58.3 3.7 %collective-permute-start.4 = (f32[4,1024]{1,0:T(4,128)S(1)}, f32[4,1024]{1,0:T(4,128)S(1)}, u32[]{:S(2)}, u32[]{:S(2)}) collective-permute-start(f32[4,1024]{1,0:T(4,128)S(1)} %all_gather.7), channel_id=1, source_target_pairs={{4,0},{0,4},{5,1},{1,5},{6,2},{2,6},{7,3},{3,7},{12,8},{8,12},{13,... | collective-permute-start | bytes 49160 | tf_op jit(solution)/shard_map/ppermute | solution.py:15
  62.0 3.4 %collective-permute-start.5 = (f32[2,4,1024]{2,1,0:T(4,128)S(1)}, f32[2,4,1024]{2,1,0:T(4,128)S(1)}, u32[]{:S(2)}, u32[]{:S(2)}) collective-permute-start(f32[2,4,1024]{2,1,0:T(4,128)S(1)} %get-tuple-element.154), channel_id=1, source_target_pairs={{24,0},{0,8},{8,16},{16,24},{25,1},{1,9},{9,17},{17,25},{26,2},{2,... | collective-permute-start | bytes 98312 | tf_op jit(solution)/shard_map/ppermute | solution.py:15
  62.1 4.3 %collective-permute-start.6 = (f32[2,4,1024]{2,1,0:T(4,128)S(1)}, f32[2,4,1024]{2,1,0:T(4,128)S(1)}, u32[]{:S(2)}, u32[]{:S(2)}) collective-permute-start(f32[2,4,1024]{2,1,0:T(4,128)S(1)} %get-tuple-element.154), channel_id=1, source_target_pairs={{16,0},{24,8},{0,16},{8,24},{17,1},{25,9},{1,17},{9,25},{18,2},{26... | collective-permute-start | bytes 98312 | tf_op jit(solution)/shard_map/ppermute | solution.py:15
  63.1 3.2 %collective-permute-start.7 = (f32[2,4,1024]{2,1,0:T(4,128)S(1)}, f32[2,4,1024]{2,1,0:T(4,128)S(1)}, u32[]{:S(2)}, u32[]{:S(2)}) collective-permute-start(f32[2,4,1024]{2,1,0:T(4,128)S(1)} %get-tuple-element.154), channel_id=1, source_target_pairs={{8,0},{16,8},{24,16},{0,24},{9,1},{17,9},{25,17},{1,25},{10,2},{18... | collective-permute-start | bytes 98312 | tf_op jit(solution)/shard_map/ppermute | solution.py:15
where the time goes:
time: 84.6 us; the launch traced here: 83.9 us
  other arithmetic  34.2 us (40%)
  blocking collectives  28.1 us (33%)
  starting transfers between devices  8.53 us (10%)
  waiting for transfers between devices  6.64 us (8%)
  local copies, waits for them, and re-layouts  4.3 us (5%)
  between operations  1.4 us (2%)
    reduce_sum x18, other arithmetic, interact(): jnp.sum(weight * separation, axis=-1)  32.3 us
    all_gather x2, blocking collectives, force_field(): tower_data = lax.all_gather(sources, 'gz', axis=1, tiled=True)  28.1 us
    ppermute x8, starting transfers between devices, passed_along(): return lax.ppermute(block, axis, route)  8.53 us
    ppermute x8, waiting for transfers between devices, passed_along(): return lax.ppermute(block, axis, route)  6.64 us
    unnamed x8, local copies, waits for them, and re-layouts  2.04 us
  transfers between devices with their start and end apart: 8, of which 7 were waited for; matrix products, arithmetic and copies ran while one was open for 1% of the time, Pallas kernels for 0%

commit v1 on v0

v1 whole, which is shorter than its diff:
```python
import functools
import math

import jax
import jax.numpy as jnp
from jax import lax
from jax.experimental import pallas as pl
from jax.experimental.pallas import tpu as pltpu
from jax.sharding import PartitionSpec as P

cutoff_square = 4.0
soften_square = 0.25
time_step = 0.1
half_step = 0.05

LANES = 128
ROWS = 8
TOGETHER = 4
TIE_SHIFT = 160
FULL = 4294967296.0


class Sizes:
    def __init__(self, lengths):
        self.lengths = lengths
        self.unit = max(set(lengths), key=lengths.count)
        step = self.unit / FULL
        self.top = cutoff_square / step**2
        self.soft = soften_square / step**2
        self.ratio = [(length / self.unit) ** 2 for length in lengths]
        self.scale = [
            (1.0 / (cutoff_square * cutoff_square)) * step * (length / FULL) for length in lengths
        ]
        self.shift = [TIE_SHIFT if length * length / 4 < cutoff_square else 0 for length in lengths]


def row_constant(values):
    row = lax.broadcasted_iota(jnp.int32, (ROWS, LANES), 0) // 2
    out = jnp.zeros((ROWS, LANES), jnp.float32)
    for c, value in enumerate(values):
        out = jnp.where(row == c, jnp.float32(value), out)
    return out


def to_steps(values, inverse):
    turns = values * inverse
    turns = turns - jnp.round(turns)
    turns = jnp.where(turns >= 0.5, -0.5, turns)
    return (turns * jnp.float32(FULL)).astype(jnp.int32)


def pair_weight(target, source, charge, sizes):
    parts = [(t - s).astype(jnp.float32) for t, s in zip(target, source)]
    squared = None
    for part, ratio in sorted(zip(parts, sizes.ratio), key=lambda item: item[1] != 1.0):
        square = part * part
        if ratio != 1.0:
            square = square * jnp.float32(ratio)
        squared = square if squared is None else squared + square
    switch = jnp.maximum(jnp.float32(sizes.top) - squared, 0.0)
    root = lax.rsqrt(squared + jnp.float32(sizes.soft))
    first = switch * root
    return parts, (first * first) * (root * charge)


def start_kernel(pos, vel, frc, chg, imass, occ, send, own, mid, mass, charge):
    live = lax.broadcasted_iota(jnp.int32, (1, 2 * LANES), 1) < occ[0, 0, 0]
    live_charge = jnp.where(live, chg[0, 0], 0.0)
    inverse = imass[0, 0]
    for h in range(2):
        cut = slice(h * LANES, (h + 1) * LANES)
        for c in range(3):
            r = slice(2 * c + h, 2 * c + h + 1)
            midway = vel[c, 0, 0] + half_step * inverse * frc[c, 0, 0]
            places = pos[c, 0, 0] + time_step * midway
            own[r, :] = places[:, cut]
            mid[r, :] = midway[:, cut]
            mass[r, :] = inverse[:, cut]
            charge[r, :] = live_charge[:, cut]
        r = slice(6 + h, 7 + h)
        own[r, :] = live_charge[:, cut]
        mid[r, :] = jnp.zeros((1, LANES), jnp.float32)
        mass[r, :] = jnp.zeros((1, LANES), jnp.float32)
        charge[r, :] = jnp.zeros((1, LANES), jnp.float32)
    block = own[...]
    for b in range(send.shape[0]):
        send[b] = block


def pack_sources(boxes, packed, steps, inverse):
    count = boxes.shape[0]
    lane = lax.broadcasted_iota(jnp.int32, (ROWS, LANES), 1)
    row = lax.broadcasted_iota(jnp.int32, (ROWS, LANES), 0)
    odd = lax.rem(row, 2) == 1
    filled = []
    for b in range(count):
        tail = boxes[b, 7:8, :]
        filled.append(jnp.max(jnp.where(tail != 0.0, lane[:1] + 1, 0)))
    position = jnp.int32(0)
    packed[0] = jnp.zeros((ROWS, LANES), jnp.float32)
    for b in range(count):
        tile = position // LANES
        begin = lax.rem(position, LANES)
        moved = pltpu.roll(boxes[b], begin, 1)
        packed[tile] = jnp.where(lane >= begin, moved, packed[tile])
        packed[tile + 1] = jnp.where(lane < begin, moved, 0.0)
        position = position + filled[b]
    tiles = (position + (LANES - 1)) // LANES
    for b in range(count):
        both = jnp.where(odd, packed[b], boxes[b])
        packed[b] = both
        steps[b] = to_steps(both, inverse)
    return tiles


def force_of(boxes, own, charge, labels, packed, steps, targets, sums, sizes):
    count = boxes.shape[0]
    inverse = row_constant([1.0 / length for length in sizes.lengths])
    tiles = pack_sources(boxes, packed, steps, inverse)
    mine = to_steps(own[...], inverse)
    columns = jnp.transpose(mine)
    for c in range(3):
        for h in range(2):
            for g in range(16):
                column = columns[8 * g : 8 * g + 8, 2 * c + h : 2 * c + h + 1]
                targets[c, 16 * h + g] = jnp.broadcast_to(column, (ROWS, LANES)) + sizes.shift[c]

    def over_targets(turn, unused):
        first = turn * TOGETHER
        target = [[targets[c, first + j] for c in range(3)] for j in range(TOGETHER)]

        def over_sources(k, totals, halves):
            totals = list(totals)
            for h in halves:
                source = [
                    jnp.broadcast_to(steps[k, 2 * c + h : 2 * c + h + 1, :], (ROWS, LANES))
                    for c in range(3)
                ]
                weight = jnp.broadcast_to(packed[k, 6 + h : 7 + h, :], (ROWS, LANES))
                for j in range(TOGETHER):
                    parts, base = pair_weight(target[j], source, weight, sizes)
                    for c in range(3):
                        totals[3 * j + c] = totals[3 * j + c] + base * parts[c]
            return tuple(totals)

        totals = (jnp.zeros((ROWS, LANES), jnp.float32),) * (3 * TOGETHER)
        totals = lax.fori_loop(0, tiles, lambda k, t: over_sources(k, t, (0, 1)), totals)
        totals = lax.fori_loop(tiles, count, lambda k, t: over_sources(k, t, (0,)), totals)
        for j in range(TOGETHER):
            for c in range(3):
                sums[c, pl.ds(pl.multiple_of((first + j) * ROWS, ROWS), ROWS), :] = totals[3 * j + c]
        return unused

    lax.fori_loop(0, 32 // TOGETHER, over_targets, 0)

    def spread(array):
        line = jnp.concatenate([array[0:1, :], array[1:2, :]], axis=1)
        return jnp.broadcast_to(line, (ROWS, 2 * LANES))

    def shifted(array):
        return pltpu.roll(pltpu.roll(array, 2 * LANES - 3, 1), 0, 1, stride=1, stride_axis=0)

    here = [spread(mine[2 * c : 2 * c + 2]) for c in range(3)]
    there = [shifted(array) for array in here]
    charge_there = shifted(spread(charge[0:2, :]))
    label = jnp.broadcast_to(labels[0, 0], (ROWS, 2 * LANES))
    slot = lax.broadcasted_iota(jnp.int32, (ROWS, 2 * LANES), 1)
    away = lax.broadcasted_iota(jnp.int32, (ROWS, 2 * LANES), 0)
    other = slot + 3 - away
    same = (shifted(label) == label) & (other >= 0) & (other < 2 * LANES) & (away < 7)
    here = [array + shift for array, shift in zip(here, sizes.shift)]
    parts, base = pair_weight(here, there, jnp.where(same, charge_there, 0.0), sizes)

    row = lax.broadcasted_iota(jnp.int32, (ROWS, LANES), 0)
    ones = jnp.ones((ROWS, LANES), jnp.float32)
    result = jnp.zeros((ROWS, LANES), jnp.float32)
    for c in range(3):
        every = lax.dot_general(
            ones, sums[c], (((1,), (1,)), ((), ())),
            precision=lax.Precision.HIGHEST, preferred_element_type=jnp.float32,
        )
        within = jnp.sum(base * parts[c], axis=0, keepdims=True)
        total = (every - within) * jnp.float32(sizes.scale[c])
        for h in range(2):
            result = jnp.where(row == 2 * c + h, total[:, h * LANES : (h + 1) * LANES], result)
    return charge[...] * result


def middle_kernel(sizes, boxes, own, mid, mass, charge, labels, send, own_out, mid_out,
                  packed, steps, targets, sums):
    force = force_of(boxes, own, charge, labels, packed, steps, targets, sums, sizes)
    kick = half_step * mass[...] * force
    midway = (mid[...] + kick) + kick
    places = own[...] + time_step * midway
    row = lax.broadcasted_iota(jnp.int32, (ROWS, LANES), 0)
    block = jnp.where(row < 6, places, own[...])
    own_out[...] = block
    mid_out[...] = midway
    for b in range(send.shape[0]):
        send[b] = block


def last_kernel(sizes, boxes, own, mid, mass, charge, labels, pos, vel, frc,
                packed, steps, targets, sums):
    force = force_of(boxes, own, charge, labels, packed, steps, targets, sums, sizes)
    velocity = mid[...] + half_step * mass[...] * force
    places = own[...]
    for c in range(3):
        for h in range(2):
            r = slice(2 * c + h, 2 * c + h + 1)
            cut = slice(h * LANES, (h + 1) * LANES)
            pos[c, 0, 0, :, cut] = places[r, :]
            vel[c, 0, 0, :, cut] = velocity[r, :]
            frc[c, 0, 0, :, cut] = force[r, :]


def cycle_offsets(cycle_size):
    if cycle_size >= 5:
        return [1, -1, 2, -2]
    return list(range(1, cycle_size))


def passed_along(block, axis, distance):
    devices = range(lax.axis_size(axis))
    route = [((i - distance) % len(devices), i) for i in devices]
    return lax.ppermute(block, axis, route)


def gather_near(copies, short, long):
    boxes = copies
    if short:
        boxes = lax.all_to_all(copies, short, 0, 0, tiled=True)
    for axis in long:
        pieces = [boxes]
        for offset in cycle_offsets(lax.axis_size(axis)):
            pieces.append(passed_along(boxes, axis, offset))
        boxes = jnp.concatenate(pieces)
    return boxes


def local(positions, velocities, forces, charges, inverse_mass, occupancy, molecule):
    axes = ("gx", "gy", "gz")
    extents = [lax.axis_size(axis) for axis in axes]
    sizes = Sizes([float(extent) for extent in extents])
    short = tuple(axis for axis, extent in zip(axes, extents) if extent < 5)
    long = tuple(axis for axis, extent in zip(axes, extents) if extent >= 5)
    copies = math.prod([1] + [extent for extent in extents if extent < 5])
    count = copies * 5 ** len(long)

    vmem = pl.BlockSpec(memory_space=pltpu.VMEM)
    smem = pl.BlockSpec(memory_space=pltpu.SMEM)
    block = jax.ShapeDtypeStruct((ROWS, LANES), jnp.float32)
    many = jax.ShapeDtypeStruct((copies, ROWS, LANES), jnp.float32)
    send, own, mid, mass, charge = pl.pallas_call(
        start_kernel,
        out_shape=(many, block, block, block, block),
        in_specs=[vmem] * 5 + [smem],
        out_specs=(vmem,) * 5,
        name="start",
    )(positions, velocities, forces, charges, inverse_mass, occupancy)

    scratch = [
        pltpu.VMEM((count + 1, ROWS, LANES), jnp.float32),
        pltpu.VMEM((count, ROWS, LANES), jnp.int32),
        pltpu.VMEM((3, 32, ROWS, LANES), jnp.int32),
        pltpu.VMEM((3, 2 * LANES, LANES), jnp.float32),
    ]
    boxes = gather_near(send, short, long)
    send, own, mid = pl.pallas_call(
        functools.partial(middle_kernel, sizes),
        out_shape=(many, block, block),
        in_specs=[vmem] * 6,
        out_specs=(vmem,) * 3,
        scratch_shapes=scratch,
        name="middle",
    )(boxes, own, mid, mass, charge, molecule)
    boxes = gather_near(send, short, long)
    whole = jax.ShapeDtypeStruct(positions.shape, jnp.float32)
    return pl.pallas_call(
        functools.partial(last_kernel, sizes),
        out_shape=(whole, whole, whole),
        in_specs=[vmem] * 6,
        out_specs=(vmem,) * 3,
        scratch_shapes=scratch,
        name="last",
    )(boxes, own, mid, mass, charge, molecule)


def solution(mesh):
    in_specs = (
        P(None, "gx", "gy", "gz", None),
        P(None, "gx", "gy", "gz", None),
        P(None, "gx", "gy", "gz", None),
        P("gx", "gy", "gz", None),
        P("gx", "gy", "gz", None),
        P("gx", "gy", "gz"),
        P("gx", "gy", "gz", None),
    )
    out_specs = (
        P(None, "gx", "gy", "gz", None),
        P(None, "gx", "gy", "gz", None),
        P(None, "gx", "gy", "gz", None),
    )
    return jax.shard_map(local, mesh=mesh, in_specs=in_specs, out_specs=out_specs, check_vma=False)
```

time: 84.6 us -> 50.3 us (0.59)
  other arithmetic: 34.2 us -> 0 us
  Pallas kernels: 0 us -> 22.6 us
  starting transfers between devices: 8.53 us -> 0 us
  waiting for transfers between devices: 6.64 us -> 0 us
  local copies, waits for them, and re-layouts: 4.3 us -> 0 us
  blocking collectives: 28.1 us -> 26.3 us
    reduce_sum x18 -> x0, other arithmetic: 32.3 us -> none  [interact(): jnp.sum(weight * separation, axis=-1)]
    all_gather x2 -> x0, blocking collectives: 28.1 us -> none  [force_field(): tower_data = lax.all_gather(sources, 'gz', axis=1, tiled=True)]
    all_to_all x0 -> x2, blocking collectives: none -> 26.3 us  [gather_near(): boxes = lax.all_to_all(copies, short, 0, 0, tiled=True)]
    pallas_call x0 -> x3, Pallas kernels: none -> 22.6 us  [the longest x1 10.6 us: local(): pl.pallas_call(functools.partial(middle_kernel, sizes), out_shape=(many,...]
    ppermute x8 -> x0, starting transfers between devices: 8.53 us -> none  [passed_along(): return lax.ppermute(block, axis, route)]
    ppermute x8 -> x0, waiting for transfers between devices: 6.64 us -> none  [passed_along(): return lax.ppermute(block, axis, route)]
    unnamed x8 -> x0, local copies, waits for them, and re-layouts: 2.04 us -> none
    reshape x3 -> x0, local copies, waits for them, and re-layouts: 1.74 us -> none  [the longest x1 0.58 us: local(): velocity.reshape(shape)]
  transfers between devices with their start and end apart: 8 -> 0, of which waited for: 7 -> 0; matrix products, arithmetic and copies ran while one was open for 1% -> 0% of each run, Pallas kernels for 0% -> 0%
where the time goes in v1:
time: 50.3 us; the launch traced here: 50.1 us
  blocking collectives  26.3 us (52%)
  Pallas kernels  22.6 us (45%)
  between operations  1.28 us (3%)
    all_to_all x2, blocking collectives, gather_near(): boxes = lax.all_to_all(copies, short, 0, 0, tiled=True)  26.3 us
    pallas_call x1, Pallas kernels, local(): pl.pallas_call(functools.partial(middle_kernel, sizes), out_shape=(many,...  10.6 us
    pallas_call x1, Pallas kernels, local(): pl.pallas_call(functools.partial(last_kernel, sizes), out_shape=(whole, w...  10.5 us
    pallas_call x1, Pallas kernels, local(): pl.pallas_call(start_kernel, out_shape=(many, block, block, block, block)...  1.42 us

profile of v1, /device:TPU:0, one launch (start us, length us, event | category | flops | bytes accessed | tf_op | source)
XLA Modules:
  0.0 50.1 jit_solution(13191934604058264021)
XLA Ops:
  1.3 1.4 %start.1 = (f32[32,8,128]{2,1,0:T(8,128)}, f32[8,128]{1,0:T(8,128)}, f32[8,128]{1,0:T(8,128)}, f32[8,128]{1,0:T(8,128)}, f32[8,128]{1,0:T(8,128)}) custom-call(f32[3,1,1,1,256]{4,3,2,1,0:T(1,128)} %pos.1, f32[3,1,1,1,256]{4,3,2,1,0:T(1,128)} %vel.1, f32[3,1,1,1,256]{4,3,2,1,0:T(1,128)} %frc.1, f32[1,1,1,256]{3,2,1,0:T(1,128)} %chg.1, ...), custom_call_target="tpu_custom_call" | custom-call | tf_op jit(solution)/shard_map/start/pallas_call | solution.py:254
  2.7 15.2 %all_to_all.10.boxes = f32[32,8,128]{2,1,0:T(8,128)} all-to-all(f32[32,8,128]{2,1,0:T(8,128)} %get-tuple-element.11), channel_id=1, replica_groups=mesh['gx'=4,'gy'=2,'gz'=4] {'gx','gy','gz'}, dimensions={0} | all-to-all | bytes 262144 | tf_op jit(solution)/shard_map/all_to_all | solution.py:232
  17.9 10.6 %middle.1 = (f32[32,8,128]{2,1,0:T(8,128)}, f32[8,128]{1,0:T(8,128)}, f32[8,128]{1,0:T(8,128)}) custom-call(f32[32,8,128]{2,1,0:T(8,128)} %all_to_all.10.boxes, f32[8,128]{1,0:T(8,128)} %get-tuple-element.12.own, f32[8,128]{1,0:T(8,128)} %get-tuple-element.13.mid, f32[8,128]{1,0:T(8,128)} %get-tuple-element.14.mass, f32[8,128]{1,0:T(8,128)} %get-tuple-element.15.charge, ...), custom_call_target="tpu_custom_call" | custom-call | tf_op jit(solution)/shard_map/middle/pallas_call | solution.py:269
  28.6 11.1 %all_to_all.11.boxes = f32[32,8,128]{2,1,0:T(8,128)} all-to-all(f32[32,8,128]{2,1,0:T(8,128)} %get-tuple-element.16), channel_id=1, replica_groups=mesh['gx'=4,'gy'=2,'gz'=4] {'gx','gy','gz'}, dimensions={0} | all-to-all | bytes 262144 | tf_op jit(solution)/shard_map/all_to_all | solution.py:232
  39.6 10.5 %last.1 = (f32[3,1,1,1,256]{4,3,2,1,0:T(1,128)}, f32[3,1,1,1,256]{4,3,2,1,0:T(1,128)}, f32[3,1,1,1,256]{4,3,2,1,0:T(1,128)}) custom-call(f32[32,8,128]{2,1,0:T(8,128)} %all_to_all.11.boxes, f32[8,128]{1,0:T(8,128)} %get-tuple-element.17.own, f32[8,128]{1,0:T(8,128)} %get-tuple-element.18.mid, f32[8,128]{1,0:T(8,128)} %get-tuple-element.14.mass, ...), custom_call_target="tpu_custom_call" | custom-call | tf_op jit(solution)/shard_map/last/pallas_call | solution.py:279

commit v2 on v1

--- a/solution.py
+++ b/solution.py
@@ -15,7 +15,7 @@
 
 LANES = 128
 ROWS = 8
-TOGETHER = 4
+UNROLL = 2
 TIE_SHIFT = 160
 FULL = 4294967296.0
 
@@ -63,16 +63,27 @@
     return parts, (first * first) * (root * charge)
 
 
-def start_kernel(pos, vel, frc, chg, imass, occ, send, own, mid, mass, charge):
+def start_kernel(pos, vel, frc, chg, imass, lab, occ, send, own, mid, mass, charge, label,
+                 pos_in, vel_in, frc_in, chg_in, imass_in, sems):
+    copies = [
+        pltpu.make_async_copy(source, target, sems.at[i])
+        for i, (source, target) in enumerate(
+            ((pos, pos_in), (vel, vel_in), (frc, frc_in), (chg, chg_in), (imass, imass_in), (lab, label))
+        )
+    ]
+    for copy in copies:
+        copy.start()
+    for copy in copies:
+        copy.wait()
     live = lax.broadcasted_iota(jnp.int32, (1, 2 * LANES), 1) < occ[0, 0, 0]
-    live_charge = jnp.where(live, chg[0, 0], 0.0)
-    inverse = imass[0, 0]
+    live_charge = jnp.where(live, chg_in[0, 0], 0.0)
+    inverse = imass_in[0, 0]
     for h in range(2):
         cut = slice(h * LANES, (h + 1) * LANES)
         for c in range(3):
             r = slice(2 * c + h, 2 * c + h + 1)
-            midway = vel[c, 0, 0] + half_step * inverse * frc[c, 0, 0]
-            places = pos[c, 0, 0] + time_step * midway
+            midway = vel_in[c, 0, 0] + half_step * inverse * frc_in[c, 0, 0]
+            places = pos_in[c, 0, 0] + time_step * midway
             own[r, :] = places[:, cut]
             mid[r, :] = midway[:, cut]
             mass[r, :] = inverse[:, cut]
@@ -87,11 +98,10 @@
         send[b] = block
 
 
-def pack_sources(boxes, packed, steps, inverse):
+def pack_sources(boxes, charges, steps, packed, inverse):
     count = boxes.shape[0]
     lane = lax.broadcasted_iota(jnp.int32, (ROWS, LANES), 1)
-    row = lax.broadcasted_iota(jnp.int32, (ROWS, LANES), 0)
-    odd = lax.rem(row, 2) == 1
+    odd = lax.rem(lax.broadcasted_iota(jnp.int32, (ROWS, LANES), 0), 2) == 1
     filled = []
     for b in range(count):
         tail = boxes[b, 7:8, :]
@@ -108,15 +118,20 @@
     tiles = (position + (LANES - 1)) // LANES
     for b in range(count):
         both = jnp.where(odd, packed[b], boxes[b])
-        packed[b] = both
-        steps[b] = to_steps(both, inverse)
-    return tiles
-
-
-def force_of(boxes, own, charge, labels, packed, steps, targets, sums, sizes):
-    count = boxes.shape[0]
+        turned = to_steps(both, inverse)
+        charges[b] = both
+        steps[b] = turned
+        charges[count + b] = pltpu.roll(both, ROWS - 1, 0)
+        steps[count + b] = pltpu.roll(turned, ROWS - 1, 0)
+    for extra in range(UNROLL):
+        charges[count + tiles + extra] = jnp.zeros((ROWS, LANES), jnp.float32)
+        steps[count + tiles + extra] = jnp.zeros((ROWS, LANES), jnp.int32)
+    return count + tiles
+
+
+def force_of(boxes, own, charge, labels, charges, steps, packed, targets, sums, sizes):
     inverse = row_constant([1.0 / length for length in sizes.lengths])
-    tiles = pack_sources(boxes, packed, steps, inverse)
+    tiles = pack_sources(boxes, charges, steps, packed, inverse)
     mine = to_steps(own[...], inverse)
     columns = jnp.transpose(mine)
     for c in range(3):
@@ -125,33 +140,30 @@
                 column = columns[8 * g : 8 * g + 8, 2 * c + h : 2 * c + h + 1]
                 targets[c, 16 * h + g] = jnp.broadcast_to(column, (ROWS, LANES)) + sizes.shift[c]
 
-    def over_targets(turn, unused):
-        first = turn * TOGETHER
-        target = [[targets[c, first + j] for c in range(3)] for j in range(TOGETHER)]
-
-        def over_sources(k, totals, halves):
-            totals = list(totals)
-            for h in halves:
-                source = [
-                    jnp.broadcast_to(steps[k, 2 * c + h : 2 * c + h + 1, :], (ROWS, LANES))
-                    for c in range(3)
-                ]
-                weight = jnp.broadcast_to(packed[k, 6 + h : 7 + h, :], (ROWS, LANES))
-                for j in range(TOGETHER):
-                    parts, base = pair_weight(target[j], source, weight, sizes)
-                    for c in range(3):
-                        totals[3 * j + c] = totals[3 * j + c] + base * parts[c]
-            return tuple(totals)
-
-        totals = (jnp.zeros((ROWS, LANES), jnp.float32),) * (3 * TOGETHER)
-        totals = lax.fori_loop(0, tiles, lambda k, t: over_sources(k, t, (0, 1)), totals)
-        totals = lax.fori_loop(tiles, count, lambda k, t: over_sources(k, t, (0,)), totals)
-        for j in range(TOGETHER):
+    for c in range(3):
+        sums[c] = jnp.zeros(sums.shape[1:], jnp.float32)
+
+    def over_sources(k, unused):
+        taken = []
+        for u in range(UNROLL):
+            tile = k * UNROLL + u
+            taken.append([
+                jnp.broadcast_to(steps[tile, 2 * c : 2 * c + 1, :], (ROWS, LANES)) for c in range(3)
+            ] + [jnp.broadcast_to(charges[tile, 6:7, :], (ROWS, LANES))])
+        for g in range(32):
+            target = [targets[c, g] for c in range(3)]
+            added = [None] * 3
+            for source in taken:
+                parts, base = pair_weight(target, source[:3], source[3], sizes)
+                for c in range(3):
+                    product = base * parts[c]
+                    added[c] = product if added[c] is None else added[c] + product
             for c in range(3):
-                sums[c, pl.ds(pl.multiple_of((first + j) * ROWS, ROWS), ROWS), :] = totals[3 * j + c]
+                rows = slice(ROWS * g, ROWS * g + ROWS)
+                sums[c, rows, :] = sums[c, rows, :] + added[c]
         return unused
 
-    lax.fori_loop(0, 32 // TOGETHER, over_targets, 0)
+    lax.fori_loop(0, (tiles + (UNROLL - 1)) // UNROLL, over_sources, 0)
 
     def spread(array):
         line = jnp.concatenate([array[0:1, :], array[1:2, :]], axis=1)
@@ -187,8 +199,8 @@
 
 
 def middle_kernel(sizes, boxes, own, mid, mass, charge, labels, send, own_out, mid_out,
-                  packed, steps, targets, sums):
-    force = force_of(boxes, own, charge, labels, packed, steps, targets, sums, sizes)
+                  charges, steps, packed, targets, sums):
+    force = force_of(boxes, own, charge, labels, charges, steps, packed, targets, sums, sizes)
     kick = half_step * mass[...] * force
     midway = (mid[...] + kick) + kick
     places = own[...] + time_step * midway
@@ -201,8 +213,8 @@
 
 
 def last_kernel(sizes, boxes, own, mid, mass, charge, labels, pos, vel, frc,
-                packed, steps, targets, sums):
-    force = force_of(boxes, own, charge, labels, packed, steps, targets, sums, sizes)
+                charges, steps, packed, targets, sums):
+    force = force_of(boxes, own, charge, labels, charges, steps, packed, targets, sums, sizes)
     velocity = mid[...] + half_step * mass[...] * force
     places = own[...]
     for c in range(3):
@@ -249,19 +261,27 @@
 
     vmem = pl.BlockSpec(memory_space=pltpu.VMEM)
     smem = pl.BlockSpec(memory_space=pltpu.SMEM)
+    small = pltpu.CompilerParams(vmem_limit_bytes=8 * 1024 * 1024)
     block = jax.ShapeDtypeStruct((ROWS, LANES), jnp.float32)
     many = jax.ShapeDtypeStruct((copies, ROWS, LANES), jnp.float32)
-    send, own, mid, mass, charge = pl.pallas_call(
+    send, own, mid, mass, charge, label = pl.pallas_call(
         start_kernel,
-        out_shape=(many, block, block, block, block),
-        in_specs=[vmem] * 5 + [smem],
-        out_specs=(vmem,) * 5,
+        out_shape=(many, block, block, block, block, jax.ShapeDtypeStruct(molecule.shape, jnp.int32)),
+        in_specs=[pl.BlockSpec(memory_space=pltpu.HBM)] * 6 + [smem],
+        out_specs=(vmem,) * 6,
+        scratch_shapes=[
+            pltpu.VMEM(array.shape, array.dtype)
+            for array in (positions, velocities, forces, charges, inverse_mass)
+        ]
+        + [pltpu.SemaphoreType.DMA((6,))],
+        compiler_params=small,
         name="start",
-    )(positions, velocities, forces, charges, inverse_mass, occupancy)
+    )(*[pltpu.with_memory_space_constraint(array, pltpu.HBM) for array in (positions, velocities, forces, charges, inverse_mass, molecule)], occupancy)
 
     scratch = [
+        pltpu.VMEM((2 * count + UNROLL, ROWS, LANES), jnp.float32),
+        pltpu.VMEM((2 * count + UNROLL, ROWS, LANES), jnp.int32),
         pltpu.VMEM((count + 1, ROWS, LANES), jnp.float32),
-        pltpu.VMEM((count, ROWS, LANES), jnp.int32),
         pltpu.VMEM((3, 32, ROWS, LANES), jnp.int32),
         pltpu.VMEM((3, 2 * LANES, LANES), jnp.float32),
     ]
@@ -272,8 +292,9 @@
         in_specs=[vmem] * 6,
         out_specs=(vmem,) * 3,
         scratch_shapes=scratch,
+        compiler_params=small,
         name="middle",
-    )(boxes, own, mid, mass, charge, molecule)
+    )(boxes, own, mid, mass, charge, label)
     boxes = gather_near(send, short, long)
     whole = jax.ShapeDtypeStruct(positions.shape, jnp.float32)
     return pl.pallas_call(
@@ -282,8 +303,9 @@
         in_specs=[vmem] * 6,
         out_specs=(vmem,) * 3,
         scratch_shapes=scratch,
+        compiler_params=small,
         name="last",
-    )(boxes, own, mid, mass, charge, molecule)
+    )(boxes, own, mid, mass, charge, label)
 
 
 def solution(mesh):

time: 50.3 us -> 41.4 us (0.82)
  Pallas kernels: 22.6 us -> 15.4 us
  blocking collectives: 26.3 us -> 24.8 us
    pallas_call x1, Pallas kernels: 10.6 us -> 6.97 us  [local(): pl.pallas_call(functools.partial(middle_kernel, sizes), out_shape=(many,...]
    pallas_call x1, Pallas kernels: 10.5 us -> 7.55 us  [local(): pl.pallas_call(functools.partial(last_kernel, sizes), out_shape=(whole, w...]
    all_to_all x2, blocking collectives: 26.3 us -> 24.8 us  [gather_near(): boxes = lax.all_to_all(copies, short, 0, 0, tiled=True)]
    pallas_call x1, Pallas kernels: 1.42 us -> 0.84 us  [local(): pl.pallas_call(start_kernel, out_shape=(many, block, block, block, block,...]
where the time goes in v2:
time: 41.4 us
  blocking collectives  24.8 us (60%)
  Pallas kernels  15.4 us (37%)
  between operations  1.3 us (3%)
    all_to_all x2, blocking collectives, gather_near(): boxes = lax.all_to_all(copies, short, 0, 0, tiled=True)  24.8 us
    pallas_call x1, Pallas kernels, local(): pl.pallas_call(functools.partial(last_kernel, sizes), out_shape=(whole, w...  7.55 us
    pallas_call x1, Pallas kernels, local(): pl.pallas_call(functools.partial(middle_kernel, sizes), out_shape=(many,...  6.97 us
    pallas_call x1, Pallas kernels, local(): pl.pallas_call(start_kernel, out_shape=(many, block, block, block, block,...  0.84 us

profile of v2, /device:TPU:0, one launch (start us, length us, event | category | flops | bytes accessed | tf_op | source)
XLA Modules:
  0.0 41.4 jit_solution(9682129307454427421)
XLA Ops:
  1.3 0.8 %start.1 = (f32[32,8,128]{2,1,0:T(8,128)S(1)}, f32[8,128]{1,0:T(8,128)S(1)}, f32[8,128]{1,0:T(8,128)S(1)}, f32[8,128]{1,0:T(8,128)S(1)}, f32[8,128]{1,0:T(8,128)S(1)}, /*index=5*/s32[1,1,1,256]{3,2,1,0:T(1,128)S(1)}) custom-call(f32[3,1,1,1,256]{4,3,2,1,0:T(1,128)} %pos.1, f32[3,1,1,1,256]{4,3,2,1,0:T(1,128)} %vel.1, f32[3,1,1,1,256]{4,3,2,1,0:T(1,128)} %frc.1, ...), custom_call_target="tpu_custom_call" | custom-call | tf_op jit(solution)/shard_map/start/pallas_call | solution.py:267
  2.1 14.9 %all_to_all.10.boxes = f32[32,8,128]{2,1,0:T(8,128)S(1)} all-to-all(f32[32,8,128]{2,1,0:T(8,128)S(1)} %get-tuple-element.12), channel_id=1, replica_groups=mesh['gx'=4,'gy'=2,'gz'=4] {'gx','gy','gz'}, dimensions={0} | all-to-all | bytes 262144 | tf_op jit(solution)/shard_map/all_to_all | solution.py:244
  17.1 7.0 %middle.1 = (f32[32,8,128]{2,1,0:T(8,128)S(1)}, f32[8,128]{1,0:T(8,128)S(1)}, f32[8,128]{1,0:T(8,128)S(1)}) custom-call(f32[32,8,128]{2,1,0:T(8,128)S(1)} %all_to_all.10.boxes, f32[8,128]{1,0:T(8,128)S(1)} %get-tuple-element.13.own, f32[8,128]{1,0:T(8,128)S(1)} %get-tuple-element.14.mid, f32[8,128]{1,0:T(8,128)S(1)} %get-tuple-element.15.mass, ...), custom_call_target="tpu_custom_call" | custom-call | tf_op jit(solution)/shard_map/middle/pallas_call | solution.py:289
  24.0 9.8 %all_to_all.11.boxes = f32[32,8,128]{2,1,0:T(8,128)S(1)} all-to-all(f32[32,8,128]{2,1,0:T(8,128)S(1)} %get-tuple-element.18), channel_id=1, replica_groups=mesh['gx'=4,'gy'=2,'gz'=4] {'gx','gy','gz'}, dimensions={0} | all-to-all | bytes 262144 | tf_op jit(solution)/shard_map/all_to_all | solution.py:244
  33.9 7.6 %last.1 = (f32[3,1,1,1,256]{4,3,2,1,0:T(1,128)}, f32[3,1,1,1,256]{4,3,2,1,0:T(1,128)}, f32[3,1,1,1,256]{4,3,2,1,0:T(1,128)}) custom-call(f32[32,8,128]{2,1,0:T(8,128)S(1)} %all_to_all.11.boxes, f32[8,128]{1,0:T(8,128)S(1)} %get-tuple-element.19.own, f32[8,128]{1,0:T(8,128)S(1)} %get-tuple-element.20.mid, f32[8,128]{1,0:T(8,128)S(1)} %get-tuple-element.15.mass, ...), custom_call_target="tpu_custom_call" | custom-call | tf_op jit(solution)/shard_map/last/pallas_call | solution.py:300

commit v3 on v2

--- a/solution.py
+++ b/solution.py
@@ -15,8 +15,7 @@
 
 LANES = 128
 ROWS = 8
-UNROLL = 2
-TIE_SHIFT = 160
+TIES = (128, 191)
 FULL = 4294967296.0
 
 
@@ -31,7 +30,7 @@
         self.scale = [
             (1.0 / (cutoff_square * cutoff_square)) * step * (length / FULL) for length in lengths
         ]
-        self.shift = [TIE_SHIFT if length * length / 4 < cutoff_square else 0 for length in lengths]
+        self.seam = [length * length / 4 < cutoff_square for length in lengths]
 
 
 def row_constant(values):
@@ -47,6 +46,16 @@
     turns = turns - jnp.round(turns)
     turns = jnp.where(turns >= 0.5, -0.5, turns)
     return (turns * jnp.float32(FULL)).astype(jnp.int32)
+
+
+def seam_shift(places, sizes):
+    row = lax.broadcasted_iota(jnp.int32, (ROWS, LANES), 0) // 2
+    shift = jnp.zeros((ROWS, LANES), jnp.int32)
+    for c, length in enumerate(sizes.lengths):
+        if sizes.seam[c]:
+            near = jnp.where(jnp.abs(places) < length / 4, TIES[0], TIES[1])
+            shift = jnp.where(row == c, near, shift)
+    return shift
 
 
 def pair_weight(target, source, charge, sizes):
@@ -98,72 +107,16 @@
         send[b] = block
 
 
-def pack_sources(boxes, charges, steps, packed, inverse):
-    count = boxes.shape[0]
-    lane = lax.broadcasted_iota(jnp.int32, (ROWS, LANES), 1)
-    odd = lax.rem(lax.broadcasted_iota(jnp.int32, (ROWS, LANES), 0), 2) == 1
-    filled = []
-    for b in range(count):
-        tail = boxes[b, 7:8, :]
-        filled.append(jnp.max(jnp.where(tail != 0.0, lane[:1] + 1, 0)))
-    position = jnp.int32(0)
-    packed[0] = jnp.zeros((ROWS, LANES), jnp.float32)
-    for b in range(count):
-        tile = position // LANES
-        begin = lax.rem(position, LANES)
-        moved = pltpu.roll(boxes[b], begin, 1)
-        packed[tile] = jnp.where(lane >= begin, moved, packed[tile])
-        packed[tile + 1] = jnp.where(lane < begin, moved, 0.0)
-        position = position + filled[b]
-    tiles = (position + (LANES - 1)) // LANES
-    for b in range(count):
-        both = jnp.where(odd, packed[b], boxes[b])
-        turned = to_steps(both, inverse)
-        charges[b] = both
-        steps[b] = turned
-        charges[count + b] = pltpu.roll(both, ROWS - 1, 0)
-        steps[count + b] = pltpu.roll(turned, ROWS - 1, 0)
-    for extra in range(UNROLL):
-        charges[count + tiles + extra] = jnp.zeros((ROWS, LANES), jnp.float32)
-        steps[count + tiles + extra] = jnp.zeros((ROWS, LANES), jnp.int32)
-    return count + tiles
-
-
-def force_of(boxes, own, charge, labels, charges, steps, packed, targets, sums, sizes):
-    inverse = row_constant([1.0 / length for length in sizes.lengths])
-    tiles = pack_sources(boxes, charges, steps, packed, inverse)
-    mine = to_steps(own[...], inverse)
-    columns = jnp.transpose(mine)
+def side_kernel(sizes, own, charge, labels, targets, band):
+    mine = to_steps(own[...], row_constant([1.0 / length for length in sizes.lengths]))
+    aim = mine + seam_shift(own[...], sizes)
+    columns = jnp.transpose(aim)
     for c in range(3):
         for h in range(2):
-            for g in range(16):
-                column = columns[8 * g : 8 * g + 8, 2 * c + h : 2 * c + h + 1]
-                targets[c, 16 * h + g] = jnp.broadcast_to(column, (ROWS, LANES)) + sizes.shift[c]
-
-    for c in range(3):
-        sums[c] = jnp.zeros(sums.shape[1:], jnp.float32)
-
-    def over_sources(k, unused):
-        taken = []
-        for u in range(UNROLL):
-            tile = k * UNROLL + u
-            taken.append([
-                jnp.broadcast_to(steps[tile, 2 * c : 2 * c + 1, :], (ROWS, LANES)) for c in range(3)
-            ] + [jnp.broadcast_to(charges[tile, 6:7, :], (ROWS, LANES))])
-        for g in range(32):
-            target = [targets[c, g] for c in range(3)]
-            added = [None] * 3
-            for source in taken:
-                parts, base = pair_weight(target, source[:3], source[3], sizes)
-                for c in range(3):
-                    product = base * parts[c]
-                    added[c] = product if added[c] is None else added[c] + product
-            for c in range(3):
-                rows = slice(ROWS * g, ROWS * g + ROWS)
-                sums[c, rows, :] = sums[c, rows, :] + added[c]
-        return unused
-
-    lax.fori_loop(0, (tiles + (UNROLL - 1)) // UNROLL, over_sources, 0)
+            for g in range(LANES // ROWS):
+                column = columns[ROWS * g : ROWS * g + ROWS, 2 * c + h : 2 * c + h + 1]
+                spot = h * (LANES // ROWS) + g
+                targets[c, spot] = jnp.broadcast_to(column, (ROWS, LANES))
 
     def spread(array):
         line = jnp.concatenate([array[0:1, :], array[1:2, :]], axis=1)
@@ -172,35 +125,115 @@
     def shifted(array):
         return pltpu.roll(pltpu.roll(array, 2 * LANES - 3, 1), 0, 1, stride=1, stride_axis=0)
 
-    here = [spread(mine[2 * c : 2 * c + 2]) for c in range(3)]
-    there = [shifted(array) for array in here]
+    here = [spread(aim[2 * c : 2 * c + 2]) for c in range(3)]
+    there = [shifted(spread(mine[2 * c : 2 * c + 2])) for c in range(3)]
     charge_there = shifted(spread(charge[0:2, :]))
     label = jnp.broadcast_to(labels[0, 0], (ROWS, 2 * LANES))
     slot = lax.broadcasted_iota(jnp.int32, (ROWS, 2 * LANES), 1)
     away = lax.broadcasted_iota(jnp.int32, (ROWS, 2 * LANES), 0)
     other = slot + 3 - away
     same = (shifted(label) == label) & (other >= 0) & (other < 2 * LANES) & (away < 7)
-    here = [array + shift for array, shift in zip(here, sizes.shift)]
     parts, base = pair_weight(here, there, jnp.where(same, charge_there, 0.0), sizes)
+    band[...] = jnp.zeros((ROWS, LANES), jnp.float32)
+    for c in range(3):
+        within = jnp.sum(base * parts[c], axis=0, keepdims=True)
+        for h in range(2):
+            band[2 * c + h : 2 * c + h + 1, :] = within[:, h * LANES : (h + 1) * LANES]
+
+
+def add_tiles(tiles, targets, sums, sizes):
+    for g in range(2 * LANES // ROWS):
+        target = [targets[c, g] for c in range(3)]
+        added = [None] * 3
+        for source, charge in tiles:
+            parts, base = pair_weight(target, source, charge, sizes)
+            for c in range(3):
+                product = base * parts[c]
+                added[c] = product if added[c] is None else added[c] + product
+        for c in range(3):
+            rows = slice(ROWS * g, ROWS * g + ROWS)
+            sums[c, rows, :] = sums[c, rows, :] + added[c]
+
+
+def force_of(boxes, charge, band, targets, steps, packed, sums, sizes):
+    count = boxes.shape[0]
+    stride = 2 if count % 2 == 0 else 1
+    inverse = row_constant([1.0 / length for length in sizes.lengths])
+    lane = lax.broadcasted_iota(jnp.int32, (ROWS, LANES), 1)
+    for c in range(3):
+        sums[c] = jnp.zeros(sums.shape[1:], jnp.float32)
+    packed[0] = jnp.zeros((ROWS, LANES), jnp.float32)
+
+    def turned(source, first, target):
+        for u in range(stride):
+            steps[target + u] = to_steps(source[first + u], inverse)
+
+    def taken(first, spot, source, half):
+        return [
+            (
+                [
+                    jnp.broadcast_to(
+                        steps[spot + u, 2 * c + half : 2 * c + half + 1, :], (ROWS, LANES)
+                    )
+                    for c in range(3)
+                ],
+                jnp.broadcast_to(source[first + u, 6 + half : 7 + half, :], (ROWS, LANES)),
+            )
+            for u in range(stride)
+        ]
+
+    def heads(k, position):
+        first = k * stride
+        spot = lax.rem(k, 2) * stride
+        add_tiles(taken(first, spot, boxes, 0), targets, sums, sizes)
+        turned(boxes, jnp.minimum(first + stride, count - stride), stride - spot)
+        for u in range(stride):
+            box = boxes[first + u]
+            filled = jnp.max(jnp.where(box[7:8, :] != 0.0, lane[:1] + 1, 0))
+            tile = position // LANES
+            begin = lax.rem(position, LANES)
+            moved = pltpu.roll(box, begin, 1)
+            packed[tile] = jnp.where(lane >= begin, moved, packed[tile])
+            packed[tile + 1] = jnp.where(lane < begin, moved, 0.0)
+            position = position + filled
+        return position
+
+    turned(boxes, 0, 0)
+    position = lax.fori_loop(0, count // stride, heads, jnp.int32(0))
+    tiles = (position + (LANES - 1)) // LANES
+    for u in range(stride):
+        packed[tiles + u] = jnp.zeros((ROWS, LANES), jnp.float32)
+
+    def tails(k, unused):
+        first = k * stride
+        spot = lax.rem(k, 2) * stride
+        add_tiles(taken(first, spot, packed, 1), targets, sums, sizes)
+        turned(packed, first + stride, stride - spot)
+        return unused
+
+    turned(packed, 0, 0)
+    lax.fori_loop(0, (tiles + stride - 1) // stride, tails, 0)
 
     row = lax.broadcasted_iota(jnp.int32, (ROWS, LANES), 0)
-    ones = jnp.ones((ROWS, LANES), jnp.float32)
+    ones = jnp.ones((ROWS, LANES), jnp.bfloat16)
     result = jnp.zeros((ROWS, LANES), jnp.float32)
     for c in range(3):
-        every = lax.dot_general(
-            ones, sums[c], (((1,), (1,)), ((), ())),
-            precision=lax.Precision.HIGHEST, preferred_element_type=jnp.float32,
-        )
-        within = jnp.sum(base * parts[c], axis=0, keepdims=True)
-        total = (every - within) * jnp.float32(sizes.scale[c])
+        left = sums[c]
+        total = jnp.zeros((ROWS, 2 * LANES), jnp.float32)
+        for piece in range(3):
+            part = left.astype(jnp.bfloat16)
+            left = left - part.astype(jnp.float32)
+            total = total + lax.dot_general(
+                ones, part, (((1,), (1,)), ((), ())), preferred_element_type=jnp.float32
+            )
         for h in range(2):
             result = jnp.where(row == 2 * c + h, total[:, h * LANES : (h + 1) * LANES], result)
-    return charge[...] * result
-
-
-def middle_kernel(sizes, boxes, own, mid, mass, charge, labels, send, own_out, mid_out,
-                  charges, steps, packed, targets, sums):
-    force = force_of(boxes, own, charge, labels, charges, steps, packed, targets, sums, sizes)
+    return charge[...] * ((result - band[...]) * row_constant(sizes.scale))
+
+
+def middle_kernel(sizes, boxes, own, mid, mass, charge, band, targets, send, own_out, mid_out,
+                  steps, packed, sums):
+    force = force_of(boxes, charge, band, targets, steps, packed, sums, sizes)
     kick = half_step * mass[...] * force
     midway = (mid[...] + kick) + kick
     places = own[...] + time_step * midway
@@ -212,9 +245,9 @@
         send[b] = block
 
 
-def last_kernel(sizes, boxes, own, mid, mass, charge, labels, pos, vel, frc,
-                charges, steps, packed, targets, sums):
-    force = force_of(boxes, own, charge, labels, charges, steps, packed, targets, sums, sizes)
+def last_kernel(sizes, boxes, own, mid, mass, charge, band, targets, pos, vel, frc,
+                steps, packed, sums):
+    force = force_of(boxes, charge, band, targets, steps, packed, sums, sizes)
     velocity = mid[...] + half_step * mass[...] * force
     places = own[...]
     for c in range(3):
@@ -278,34 +311,50 @@
         name="start",
     )(*[pltpu.with_memory_space_constraint(array, pltpu.HBM) for array in (positions, velocities, forces, charges, inverse_mass, molecule)], occupancy)
 
+    pairs = 2 * LANES * LANES * 2 * count
     scratch = [
-        pltpu.VMEM((2 * count + UNROLL, ROWS, LANES), jnp.float32),
-        pltpu.VMEM((2 * count + UNROLL, ROWS, LANES), jnp.int32),
-        pltpu.VMEM((count + 1, ROWS, LANES), jnp.float32),
-        pltpu.VMEM((3, 32, ROWS, LANES), jnp.int32),
+        pltpu.VMEM((4, ROWS, LANES), jnp.int32),
+        pltpu.VMEM((count + 4, ROWS, LANES), jnp.float32),
         pltpu.VMEM((3, 2 * LANES, LANES), jnp.float32),
     ]
+    cost = pl.CostEstimate(flops=26 * pairs, bytes_accessed=64 * pairs // LANES, transcendentals=pairs)
+
+    def beside(own):
+        return pl.pallas_call(
+            functools.partial(side_kernel, sizes),
+            out_shape=(jax.ShapeDtypeStruct((3, 2 * LANES // ROWS, ROWS, LANES), jnp.int32), block),
+            in_specs=[vmem] * 3,
+            out_specs=(vmem,) * 2,
+            compiler_params=small,
+            cost_estimate=pl.CostEstimate(flops=4_000_000, bytes_accessed=400_000, transcendentals=2048),
+            name="side",
+        )(own, charge, label)
+
+    targets, band = beside(own)
     boxes = gather_near(send, short, long)
     send, own, mid = pl.pallas_call(
         functools.partial(middle_kernel, sizes),
         out_shape=(many, block, block),
-        in_specs=[vmem] * 6,
+        in_specs=[vmem] * 7,
         out_specs=(vmem,) * 3,
         scratch_shapes=scratch,
         compiler_params=small,
+        cost_estimate=cost,
         name="middle",
-    )(boxes, own, mid, mass, charge, label)
+    )(boxes, own, mid, mass, charge, band, targets)
+    targets, band = beside(own)
     boxes = gather_near(send, short, long)
     whole = jax.ShapeDtypeStruct(positions.shape, jnp.float32)
     return pl.pallas_call(
         functools.partial(last_kernel, sizes),
         out_shape=(whole, whole, whole),
-        in_specs=[vmem] * 6,
+        in_specs=[vmem] * 7,
         out_specs=(vmem,) * 3,
         scratch_shapes=scratch,
         compiler_params=small,
+        cost_estimate=cost,
         name="last",
-    )(boxes, own, mid, mass, charge, label)
+    )(boxes, own, mid, mass, charge, band, targets)
 
 
 def solution(mesh):

time: 41.4 us -> 47.8 us (1.15); the launches traced: 41.4 us -> 47.3 us
  blocking collectives: 24.8 us -> 0 us
  waiting for transfers between devices: 0 us -> 14.8 us
  starting transfers between devices: 0 us -> 9.89 us
  Pallas kernels: 15.4 us -> 21.2 us
    all_to_all x2 -> x0, blocking collectives: 24.8 us -> none  [gather_near(): boxes = lax.all_to_all(copies, short, 0, 0, tiled=True)]
    all_to_all x0 -> x2, waiting for transfers between devices: none -> 14.8 us  [gather_near(): boxes = lax.all_to_all(copies, short, 0, 0, tiled=True)]
    all_to_all x0 -> x2, starting transfers between devices: none -> 9.89 us  [gather_near(): boxes = lax.all_to_all(copies, short, 0, 0, tiled=True)]
    pallas_call x1, Pallas kernels: 6.97 us -> 9.55 us  [local(): pl.pallas_call(functools.partial(middle_kernel, sizes), out_shape=(many,...]
    pallas_call x1, Pallas kernels: 7.55 us -> 9.47 us  [local(): pl.pallas_call(functools.partial(last_kernel, sizes), out_shape=(whole, w...]
    pallas_call x0 -> x2, Pallas kernels: none -> 0.74 us  [beside(): pl.pallas_call(functools.partial(side_kernel, sizes), out_shape=(jax.Shap...]
    pallas_call x1, Pallas kernels: 0.84 us -> 1.49 us  [local(): pl.pallas_call(start_kernel, out_shape=(many, block, block, block, block,...]
  transfers between devices with their start and end apart: 0 -> 2, of which waited for: 0 -> 2; matrix products, arithmetic and copies ran while one was open for 0% -> 0% of each run, Pallas kernels for 0% -> 2%
where the time goes in v3:
time: 47.8 us; the launch traced here: 47.3 us
  Pallas kernels  21.2 us (44%)
  waiting for transfers between devices  14.8 us (31%)
  starting transfers between devices  9.89 us (21%)
  between operations  1.32 us (3%)
    all_to_all x2, waiting for transfers between devices, gather_near(): boxes = lax.all_to_all(copies, short, 0, 0, tiled=True)  14.8 us
    all_to_all x2, starting transfers between devices, gather_near(): boxes = lax.all_to_all(copies, short, 0, 0, tiled=True)  9.89 us
    pallas_call x1, Pallas kernels, local(): pl.pallas_call(functools.partial(middle_kernel, sizes), out_shape=(many,...  9.55 us
    pallas_call x1, Pallas kernels, local(): pl.pallas_call(functools.partial(last_kernel, sizes), out_shape=(whole, w...  9.47 us
    pallas_call x1, Pallas kernels, local(): pl.pallas_call(start_kernel, out_shape=(many, block, block, block, block,...  1.49 us
  transfers between devices with their start and end apart: 2, of which 2 were waited for; matrix products, arithmetic and copies ran while one was open for 0% of the time, Pallas kernels for 2%

profile of v3, /device:TPU:0, one launch (start us, length us, event | category | flops | bytes accessed | tf_op | source)
XLA Modules:
  0.0 47.3 jit_solution(9054491324072604867)
XLA Ops:
  1.3 1.5 %start.1 = (f32[32,8,128]{2,1,0:T(8,128)}, f32[8,128]{1,0:T(8,128)S(1)}, f32[8,128]{1,0:T(8,128)S(1)}, f32[8,128]{1,0:T(8,128)S(1)}, f32[8,128]{1,0:T(8,128)S(1)}, /*index=5*/s32[1,1,1,256]{3,2,1,0:T(1,128)S(1)}) custom-call(f32[3,1,1,1,256]{4,3,2,1,0:T(1,128)} %pos.1, f32[3,1,1,1,256]{4,3,2,1,0:T(1,128)} %vel.1, f32[3,1,1,1,256]{4,3,2,1,0:T(1,128)} %frc.1, ...), custom_call_target="tpu_custom_call" | custom-call | tf_op jit(solution)/shard_map/start/pallas_call | solution.py:300
  2.8 7.3 %all-to-all-start = ((f32[32,8,128]{2,1,0:T(8,128)}), f32[32,8,128]{2,1,0:T(8,128)S(1)}, u32[]{:S(2)}, u32[]{:S(2)}) async-start(f32[32,8,128]{2,1,0:T(8,128)} %get-tuple-element.16), calls=%async_computation | async-start | bytes 262144 | tf_op jit(solution)/shard_map/all_to_all | solution.py:277
  10.1 0.4 side.2
  10.5 7.4 %all-to-all-done.boxes = f32[32,8,128]{2,1,0:T(8,128)S(1)} async-done(((f32[32,8,128]{2,1,0:T(8,128)}), f32[32,8,128]{2,1,0:T(8,128)S(1)}, u32[]{:S(2)}, u32[]{:S(2)}) %all-to-all-start) | async-done | bytes 131104 | tf_op jit(solution)/shard_map/all_to_all | solution.py:277
  17.9 9.5 %middle.1 = (f32[32,8,128]{2,1,0:T(8,128)}, f32[8,128]{1,0:T(8,128)S(1)}, f32[8,128]{1,0:T(8,128)S(1)}) custom-call(f32[32,8,128]{2,1,0:T(8,128)S(1)} %all-to-all-done.boxes, f32[8,128]{1,0:T(8,128)S(1)} %get-tuple-element.17.own, f32[8,128]{1,0:T(8,128)S(1)} %get-tuple-element.18.mid, f32[8,128]{1,0:T(8,128)S(1)} %get-tuple-element.19.mass, ...), custom_call_target="tpu_custom_call" | custom-call | flops 54525952 | bytes 1048576 | tf_op jit(solution)/shard_map/middle/pallas_call | solution.py:335
  27.5 2.6 %all-to-all-start.1 = ((f32[32,8,128]{2,1,0:T(8,128)}), f32[32,8,128]{2,1,0:T(8,128)S(1)}, u32[]{:S(2)}, u32[]{:S(2)}) async-start(f32[32,8,128]{2,1,0:T(8,128)} %get-tuple-element.24), calls=%async_computation.1 | async-start | bytes 262144 | tf_op jit(solution)/shard_map/all_to_all | solution.py:277
  30.0 0.4 side.3
  30.4 7.4 %all-to-all-done.1.boxes = f32[32,8,128]{2,1,0:T(8,128)S(1)} async-done(((f32[32,8,128]{2,1,0:T(8,128)}), f32[32,8,128]{2,1,0:T(8,128)S(1)}, u32[]{:S(2)}, u32[]{:S(2)}) %all-to-all-start.1) | async-done | bytes 131104 | tf_op jit(solution)/shard_map/all_to_all | solution.py:277
  37.8 9.5 %last.1 = (f32[3,1,1,1,256]{4,3,2,1,0:T(1,128)}, f32[3,1,1,1,256]{4,3,2,1,0:T(1,128)}, f32[3,1,1,1,256]{4,3,2,1,0:T(1,128)}) custom-call(f32[32,8,128]{2,1,0:T(8,128)S(1)} %all-to-all-done.1.boxes, f32[8,128]{1,0:T(8,128)S(1)} %get-tuple-element.25.own, f32[8,128]{1,0:T(8,128)S(1)} %get-tuple-element.26.mid, f32[8,128]{1,0:T(8,128)S(1)} %get-tuple-element.19.mass, ...), custom_call_target="tpu_custom_call" | custom-call | flops 54525952 | bytes 1048576 | tf_op jit(solution)/shard_map/last/pallas_call | solution.py:348
Async XLA Ops:
  2.8 15.1 %all-to-all-start = ((f32[32,8,128]{2,1,0:T(8,128)}), f32[32,8,128]{2,1,0:T(8,128)S(1)}, u32[]{:S(2)}, u32[]{:S(2)}) async-start(f32[32,8,128]{2,1,0:T(8,128)} %get-tuple-element.16), calls=%async_computation | async-start | bytes 262144 | tf_op jit(solution)/shard_map/all_to_all | solution.py:277
  27.5 10.4 %all-to-all-start.1 = ((f32[32,8,128]{2,1,0:T(8,128)}), f32[32,8,128]{2,1,0:T(8,128)S(1)}, u32[]{:S(2)}, u32[]{:S(2)}) async-start(f32[32,8,128]{2,1,0:T(8,128)} %get-tuple-element.24), calls=%async_computation.1 | async-start | bytes 262144 | tf_op jit(solution)/shard_map/all_to_all | solution.py:277

commit v4 on v3

--- a/solution.py
+++ b/solution.py
@@ -107,7 +107,7 @@
         send[b] = block
 
 
-def side_kernel(sizes, own, charge, labels, targets, band):
+def prepare(own, charge, labels, targets, sizes):
     mine = to_steps(own[...], row_constant([1.0 / length for length in sizes.lengths]))
     aim = mine + seam_shift(own[...], sizes)
     columns = jnp.transpose(aim)
@@ -134,11 +134,7 @@
     other = slot + 3 - away
     same = (shifted(label) == label) & (other >= 0) & (other < 2 * LANES) & (away < 7)
     parts, base = pair_weight(here, there, jnp.where(same, charge_there, 0.0), sizes)
-    band[...] = jnp.zeros((ROWS, LANES), jnp.float32)
-    for c in range(3):
-        within = jnp.sum(base * parts[c], axis=0, keepdims=True)
-        for h in range(2):
-            band[2 * c + h : 2 * c + h + 1, :] = within[:, h * LANES : (h + 1) * LANES]
+    return [jnp.sum(base * parts[c], axis=0, keepdims=True) for c in range(3)]
 
 
 def add_tiles(tiles, targets, sums, sizes):
@@ -155,11 +151,12 @@
             sums[c, rows, :] = sums[c, rows, :] + added[c]
 
 
-def force_of(boxes, charge, band, targets, steps, packed, sums, sizes):
+def force_of(boxes, own, charge, labels, steps, packed, offsets, targets, sums, sizes):
     count = boxes.shape[0]
     stride = 2 if count % 2 == 0 else 1
     inverse = row_constant([1.0 / length for length in sizes.lengths])
     lane = lax.broadcasted_iota(jnp.int32, (ROWS, LANES), 1)
+    within = prepare(own, charge, labels, targets, sizes)
     for c in range(3):
         sums[c] = jnp.zeros(sums.shape[1:], jnp.float32)
     packed[0] = jnp.zeros((ROWS, LANES), jnp.float32)
@@ -182,24 +179,29 @@
             for u in range(stride)
         ]
 
-    def heads(k, position):
+    def heads(k, unused):
         first = k * stride
         spot = lax.rem(k, 2) * stride
         add_tiles(taken(first, spot, boxes, 0), targets, sums, sizes)
         turned(boxes, jnp.minimum(first + stride, count - stride), stride - spot)
         for u in range(stride):
             box = boxes[first + u]
-            filled = jnp.max(jnp.where(box[7:8, :] != 0.0, lane[:1] + 1, 0))
+            position = offsets[first + u]
             tile = position // LANES
             begin = lax.rem(position, LANES)
             moved = pltpu.roll(box, begin, 1)
-            packed[tile] = jnp.where(lane >= begin, moved, packed[tile])
+            pltpu.store(packed.at[tile], moved, mask=lane >= begin)
             packed[tile + 1] = jnp.where(lane < begin, moved, 0.0)
-            position = position + filled
-        return position
+        return unused
 
     turned(boxes, 0, 0)
-    position = lax.fori_loop(0, count // stride, heads, jnp.int32(0))
+    position = jnp.int32(0)
+    last_live = jnp.max(jnp.where(boxes[:, 7, :] != 0.0, lane[:1].astype(jnp.float32) + 1.0, 0.0), axis=1, keepdims=True)
+    filled = last_live.astype(jnp.int32)
+    for b in range(count):
+        offsets[b] = position
+        position = position + filled[b, 0]
+    lax.fori_loop(0, count // stride, heads, 0)
     tiles = (position + (LANES - 1)) // LANES
     for u in range(stride):
         packed[tiles + u] = jnp.zeros((ROWS, LANES), jnp.float32)
@@ -226,14 +228,15 @@
             total = total + lax.dot_general(
                 ones, part, (((1,), (1,)), ((), ())), preferred_element_type=jnp.float32
             )
+        total = (total - within[c]) * jnp.float32(sizes.scale[c])
         for h in range(2):
             result = jnp.where(row == 2 * c + h, total[:, h * LANES : (h + 1) * LANES], result)
-    return charge[...] * ((result - band[...]) * row_constant(sizes.scale))
-
-
-def middle_kernel(sizes, boxes, own, mid, mass, charge, band, targets, send, own_out, mid_out,
-                  steps, packed, sums):
-    force = force_of(boxes, charge, band, targets, steps, packed, sums, sizes)
+    return charge[...] * result
+
+
+def middle_kernel(sizes, boxes, own, mid, mass, charge, labels, send, own_out, mid_out,
+                  steps, packed, offsets, targets, sums):
+    force = force_of(boxes, own, charge, labels, steps, packed, offsets, targets, sums, sizes)
     kick = half_step * mass[...] * force
     midway = (mid[...] + kick) + kick
     places = own[...] + time_step * midway
@@ -245,9 +248,9 @@
         send[b] = block
 
 
-def last_kernel(sizes, boxes, own, mid, mass, charge, band, targets, pos, vel, frc,
-                steps, packed, sums):
-    force = force_of(boxes, charge, band, targets, steps, packed, sums, sizes)
+def last_kernel(sizes, boxes, own, mid, mass, charge, labels, pos, vel, frc,
+                steps, packed, offsets, targets, sums):
+    force = force_of(boxes, own, charge, labels, steps, packed, offsets, targets, sums, sizes)
     velocity = mid[...] + half_step * mass[...] * force
     places = own[...]
     for c in range(3):
@@ -315,46 +318,35 @@
     scratch = [
         pltpu.VMEM((4, ROWS, LANES), jnp.int32),
         pltpu.VMEM((count + 4, ROWS, LANES), jnp.float32),
+        pltpu.SMEM((count,), jnp.int32),
+        pltpu.VMEM((3, 2 * LANES // ROWS, ROWS, LANES), jnp.int32),
         pltpu.VMEM((3, 2 * LANES, LANES), jnp.float32),
     ]
     cost = pl.CostEstimate(flops=26 * pairs, bytes_accessed=64 * pairs // LANES, transcendentals=pairs)
 
-    def beside(own):
-        return pl.pallas_call(
-            functools.partial(side_kernel, sizes),
-            out_shape=(jax.ShapeDtypeStruct((3, 2 * LANES // ROWS, ROWS, LANES), jnp.int32), block),
-            in_specs=[vmem] * 3,
-            out_specs=(vmem,) * 2,
-            compiler_params=small,
-            cost_estimate=pl.CostEstimate(flops=4_000_000, bytes_accessed=400_000, transcendentals=2048),
-            name="side",
-        )(own, charge, label)
-
-    targets, band = beside(own)
     boxes = gather_near(send, short, long)
     send, own, mid = pl.pallas_call(
         functools.partial(middle_kernel, sizes),
         out_shape=(many, block, block),
-        in_specs=[vmem] * 7,
+        in_specs=[vmem] * 6,
         out_specs=(vmem,) * 3,
         scratch_shapes=scratch,
         compiler_params=small,
         cost_estimate=cost,
         name="middle",
-    )(boxes, own, mid, mass, charge, band, targets)
-    targets, band = beside(own)
+    )(boxes, own, mid, mass, charge, label)
     boxes = gather_near(send, short, long)
     whole = jax.ShapeDtypeStruct(positions.shape, jnp.float32)
     return pl.pallas_call(
         functools.partial(last_kernel, sizes),
         out_shape=(whole, whole, whole),
-        in_specs=[vmem] * 7,
+        in_specs=[vmem] * 6,
         out_specs=(vmem,) * 3,
         scratch_shapes=scratch,
         compiler_params=small,
         cost_estimate=cost,
         name="last",
-    )(boxes, own, mid, mass, charge, band, targets)
+    )(boxes, own, mid, mass, charge, label)
 
 
 def solution(mesh):

time: 47.8 us -> 40.4 us (0.85)
  blocking collectives: 0 us -> 24.8 us
  waiting for transfers between devices: 14.8 us -> 0 us
  starting transfers between devices: 9.89 us -> 0 us
  Pallas kernels: 21.2 us -> 14.2 us
    all_to_all x0 -> x2, blocking collectives: none -> 24.8 us  [gather_near(): boxes = lax.all_to_all(copies, short, 0, 0, tiled=True)]
    all_to_all x2 -> x0, waiting for transfers between devices: 14.8 us -> none  [gather_near(): boxes = lax.all_to_all(copies, short, 0, 0, tiled=True)]
    all_to_all x2 -> x0, starting transfers between devices: 9.89 us -> none  [gather_near(): boxes = lax.all_to_all(copies, short, 0, 0, tiled=True)]
    pallas_call x1, Pallas kernels: 9.55 us -> 6.36 us  [local(): pl.pallas_call(functools.partial(middle_kernel, sizes), out_shape=(many,...]
    pallas_call x1, Pallas kernels: 9.47 us -> 6.96 us  [local(): pl.pallas_call(functools.partial(last_kernel, sizes), out_shape=(whole, w...]
    pallas_call x2 -> x0, Pallas kernels: 0.74 us -> none  [beside(): pl.pallas_call(functools.partial(side_kernel, sizes), out_shape=(jax.Shap...]
    pallas_call x1, Pallas kernels: 1.49 us -> 0.84 us  [local(): pl.pallas_call(start_kernel, out_shape=(many, block, block, block, block,...]
  transfers between devices with their start and end apart: 2 -> 0, of which waited for: 2 -> 0; matrix products, arithmetic and copies ran while one was open for 0% -> 0% of each run, Pallas kernels for 2% -> 0%
where the time goes in v4:
time: 40.4 us; the launch traced here: 40.2 us
  blocking collectives  24.8 us (61%)
  Pallas kernels  14.2 us (35%)
  between operations  1.3 us (3%)
    all_to_all x2, blocking collectives, gather_near(): boxes = lax.all_to_all(copies, short, 0, 0, tiled=True)  24.8 us
    pallas_call x1, Pallas kernels, local(): pl.pallas_call(functools.partial(last_kernel, sizes), out_shape=(whole, w...  6.96 us
    pallas_call x1, Pallas kernels, local(): pl.pallas_call(functools.partial(middle_kernel, sizes), out_shape=(many,...  6.36 us
    pallas_call x1, Pallas kernels, local(): pl.pallas_call(start_kernel, out_shape=(many, block, block, block, block,...  0.84 us

profile of v4, /device:TPU:0, one launch (start us, length us, event | category | flops | bytes accessed | tf_op | source)
XLA Modules:
  0.0 40.2 jit_solution(6024657091731582935)
XLA Ops:
  1.3 0.8 %start.1 = (f32[32,8,128]{2,1,0:T(8,128)S(1)}, f32[8,128]{1,0:T(8,128)S(1)}, f32[8,128]{1,0:T(8,128)S(1)}, f32[8,128]{1,0:T(8,128)S(1)}, f32[8,128]{1,0:T(8,128)S(1)}, /*index=5*/s32[1,1,1,256]{3,2,1,0:T(1,128)S(1)}) custom-call(f32[3,1,1,1,256]{4,3,2,1,0:T(1,128)} %pos.1, f32[3,1,1,1,256]{4,3,2,1,0:T(1,128)} %vel.1, f32[3,1,1,1,256]{4,3,2,1,0:T(1,128)} %frc.1, ...), custom_call_target="tpu_custom_call" | custom-call | tf_op jit(solution)/shard_map/start/pallas_call | solution.py:303
  2.1 14.9 %all_to_all.10.boxes = f32[32,8,128]{2,1,0:T(8,128)S(1)} all-to-all(f32[32,8,128]{2,1,0:T(8,128)S(1)} %get-tuple-element.12), channel_id=1, replica_groups=mesh['gx'=4,'gy'=2,'gz'=4] {'gx','gy','gz'}, dimensions={0} | all-to-all | bytes 262144 | tf_op jit(solution)/shard_map/all_to_all | solution.py:280
  17.1 6.4 %middle.1 = (f32[32,8,128]{2,1,0:T(8,128)S(1)}, f32[8,128]{1,0:T(8,128)S(1)}, f32[8,128]{1,0:T(8,128)S(1)}) custom-call(f32[32,8,128]{2,1,0:T(8,128)S(1)} %all_to_all.10.boxes, f32[8,128]{1,0:T(8,128)S(1)} %get-tuple-element.13.own, f32[8,128]{1,0:T(8,128)S(1)} %get-tuple-element.14.mid, f32[8,128]{1,0:T(8,128)S(1)} %get-tuple-element.15.mass, ...), custom_call_target="tpu_custom_call" | custom-call | flops 54525952 | bytes 1048576 | tf_op jit(solution)/shard_map/middle/pallas_call | solution.py:328
  23.4 9.8 %all_to_all.11.boxes = f32[32,8,128]{2,1,0:T(8,128)S(1)} all-to-all(f32[32,8,128]{2,1,0:T(8,128)S(1)} %get-tuple-element.18), channel_id=1, replica_groups=mesh['gx'=4,'gy'=2,'gz'=4] {'gx','gy','gz'}, dimensions={0} | all-to-all | bytes 262144 | tf_op jit(solution)/shard_map/all_to_all | solution.py:280
  33.3 7.0 %last.1 = (f32[3,1,1,1,256]{4,3,2,1,0:T(1,128)}, f32[3,1,1,1,256]{4,3,2,1,0:T(1,128)}, f32[3,1,1,1,256]{4,3,2,1,0:T(1,128)}) custom-call(f32[32,8,128]{2,1,0:T(8,128)S(1)} %all_to_all.11.boxes, f32[8,128]{1,0:T(8,128)S(1)} %get-tuple-element.19.own, f32[8,128]{1,0:T(8,128)S(1)} %get-tuple-element.20.mid, f32[8,128]{1,0:T(8,128)S(1)} %get-tuple-element.15.mass, ...), custom_call_target="tpu_custom_call" | custom-call | flops 54525952 | bytes 1048576 | tf_op jit(solution)/shard_map/last/pallas_call | solution.py:340

commit v5 on v4

--- a/solution.py
+++ b/solution.py
@@ -151,70 +151,80 @@
             sums[c, rows, :] = sums[c, rows, :] + added[c]
 
 
-def force_of(boxes, own, charge, labels, steps, packed, offsets, targets, sums, sizes):
-    count = boxes.shape[0]
+def force_of(charges, places, per, own, charge, labels, steps, packed, packed_charges, offsets,
+             targets, sums, sizes):
+    count = charges.shape[0] // ROWS
     stride = 2 if count % 2 == 0 else 1
-    inverse = row_constant([1.0 / length for length in sizes.lengths])
     lane = lax.broadcasted_iota(jnp.int32, (ROWS, LANES), 1)
     within = prepare(own, charge, labels, targets, sizes)
     for c in range(3):
         sums[c] = jnp.zeros(sums.shape[1:], jnp.float32)
-    packed[0] = jnp.zeros((ROWS, LANES), jnp.float32)
-
-    def turned(source, first, target):
-        for u in range(stride):
-            steps[target + u] = to_steps(source[first + u], inverse)
-
-    def taken(first, spot, source, half):
-        return [
-            (
-                [
-                    jnp.broadcast_to(
-                        steps[spot + u, 2 * c + half : 2 * c + half + 1, :], (ROWS, LANES)
-                    )
-                    for c in range(3)
-                ],
-                jnp.broadcast_to(source[first + u, 6 + half : 7 + half, :], (ROWS, LANES)),
-            )
-            for u in range(stride)
+
+    inverses = {}
+    for k in range(pl.cdiv(places.shape[0], ROWS)):
+        begin = (ROWS * k) % per
+        if begin not in inverses:
+            axis = lax.rem(lax.broadcasted_iota(jnp.int32, (ROWS, LANES), 0) + begin, per) // 2
+            inverse = jnp.zeros((ROWS, LANES), jnp.float32)
+            for c, length in enumerate(sizes.lengths):
+                inverse = jnp.where(axis == c, jnp.float32(1.0 / length), inverse)
+            inverses[begin] = inverse
+        size = min(ROWS, places.shape[0] - ROWS * k)
+        rows = slice(ROWS * k, ROWS * k + size)
+        steps[rows, :] = to_steps(places[rows, :], inverses[begin][:size])
+
+    def one(ref, row):
+        return jnp.broadcast_to(ref[pl.ds(row, 1), :], (ROWS, LANES))
+
+    def heads(k, unused):
+        boxes = [k * stride + u for u in range(stride)]
+        tiles = [
+            ([one(steps, b * per + 2 * c) for c in range(3)], one(charges, b * ROWS + 6))
+            for b in boxes
         ]
-
-    def heads(k, unused):
-        first = k * stride
-        spot = lax.rem(k, 2) * stride
-        add_tiles(taken(first, spot, boxes, 0), targets, sums, sizes)
-        turned(boxes, jnp.minimum(first + stride, count - stride), stride - spot)
-        for u in range(stride):
-            box = boxes[first + u]
-            position = offsets[first + u]
+        add_tiles(tiles, targets, sums, sizes)
+        for b in boxes:
+            position = offsets[b]
             tile = position // LANES
             begin = lax.rem(position, LANES)
+            late = lane >= begin
+            moved = pltpu.roll(steps[pl.ds(b * per, ROWS), :], begin, 1)
+            pltpu.store(packed.at[tile], moved, mask=late)
+            packed[tile + 1] = moved
+            box = charges[pl.ds(pl.multiple_of(b * ROWS, ROWS), ROWS), :]
             moved = pltpu.roll(box, begin, 1)
-            pltpu.store(packed.at[tile], moved, mask=lane >= begin)
-            packed[tile + 1] = jnp.where(lane < begin, moved, 0.0)
+            pltpu.store(packed_charges.at[tile], moved, mask=late)
+            packed_charges[tile + 1] = jnp.where(late, 0.0, moved)
         return unused
 
-    turned(boxes, 0, 0)
+    live = jnp.where(
+        charges[pl.ds(7, count, stride=ROWS), :] != 0.0, lane[:1].astype(jnp.float32) + 1.0, 0.0
+    )
+    filled = jnp.max(live, axis=1, keepdims=True).astype(jnp.int32)
     position = jnp.int32(0)
-    last_live = jnp.max(jnp.where(boxes[:, 7, :] != 0.0, lane[:1].astype(jnp.float32) + 1.0, 0.0), axis=1, keepdims=True)
-    filled = last_live.astype(jnp.int32)
     for b in range(count):
         offsets[b] = position
         position = position + filled[b, 0]
     lax.fori_loop(0, count // stride, heads, 0)
-    tiles = (position + (LANES - 1)) // LANES
+    filled_tiles = (position + (LANES - 1)) // LANES
     for u in range(stride):
-        packed[tiles + u] = jnp.zeros((ROWS, LANES), jnp.float32)
+        packed_charges[filled_tiles + u] = jnp.zeros((ROWS, LANES), jnp.float32)
 
     def tails(k, unused):
-        first = k * stride
-        spot = lax.rem(k, 2) * stride
-        add_tiles(taken(first, spot, packed, 1), targets, sums, sizes)
-        turned(packed, first + stride, stride - spot)
+        tiles = [
+            (
+                [
+                    jnp.broadcast_to(packed[t, 2 * c + 1 : 2 * c + 2, :], (ROWS, LANES))
+                    for c in range(3)
+                ],
+                jnp.broadcast_to(packed_charges[t, 7:8, :], (ROWS, LANES)),
+            )
+            for t in [k * stride + u for u in range(stride)]
+        ]
+        add_tiles(tiles, targets, sums, sizes)
         return unused
 
-    turned(packed, 0, 0)
-    lax.fori_loop(0, (tiles + stride - 1) // stride, tails, 0)
+    lax.fori_loop(0, (filled_tiles + stride - 1) // stride, tails, 0)
 
     row = lax.broadcasted_iota(jnp.int32, (ROWS, LANES), 0)
     ones = jnp.ones((ROWS, LANES), jnp.bfloat16)
@@ -234,9 +244,8 @@
     return charge[...] * result
 
 
-def middle_kernel(sizes, boxes, own, mid, mass, charge, labels, send, own_out, mid_out,
-                  steps, packed, offsets, targets, sums):
-    force = force_of(boxes, own, charge, labels, steps, packed, offsets, targets, sums, sizes)
+def middle_kernel(sizes, boxes, own, mid, mass, charge, labels, send, own_out, mid_out, *scratch):
+    force = force_of(boxes, boxes, ROWS, own, charge, labels, *scratch, sizes)
     kick = half_step * mass[...] * force
     midway = (mid[...] + kick) + kick
     places = own[...] + time_step * midway
@@ -244,13 +253,18 @@
     block = jnp.where(row < 6, places, own[...])
     own_out[...] = block
     mid_out[...] = midway
-    for b in range(send.shape[0]):
-        send[b] = block
-
-
-def last_kernel(sizes, boxes, own, mid, mass, charge, labels, pos, vel, frc,
-                steps, packed, offsets, targets, sums):
-    force = force_of(boxes, own, charge, labels, steps, packed, offsets, targets, sums, sizes)
+    rows = send.shape[0]
+    for k in range(pl.cdiv(rows, ROWS)):
+        begin = (ROWS * k) % 6
+        early = block if begin == 0 else pltpu.roll(block, ROWS - begin, 0)
+        late = pltpu.roll(block, (6 - begin) % ROWS, 0)
+        twice = jnp.where(row < 6 - begin, early, late)
+        size = min(ROWS, rows - ROWS * k)
+        send[ROWS * k : ROWS * k + size, :] = twice[:size]
+
+
+def last_kernel(sizes, boxes, places_in, own, mid, mass, charge, labels, pos, vel, frc, *scratch):
+    force = force_of(boxes, places_in, 6, own, charge, labels, *scratch, sizes)
     velocity = mid[...] + half_step * mass[...] * force
     places = own[...]
     for c in range(3):
@@ -316,7 +330,8 @@
 
     pairs = 2 * LANES * LANES * 2 * count
     scratch = [
-        pltpu.VMEM((4, ROWS, LANES), jnp.int32),
+        pltpu.VMEM((ROWS * (count + 1), LANES), jnp.int32),
+        pltpu.VMEM((count + 4, ROWS, LANES), jnp.int32),
         pltpu.VMEM((count + 4, ROWS, LANES), jnp.float32),
         pltpu.SMEM((count,), jnp.int32),
         pltpu.VMEM((3, 2 * LANES // ROWS, ROWS, LANES), jnp.int32),
@@ -324,10 +339,10 @@
     ]
     cost = pl.CostEstimate(flops=26 * pairs, bytes_accessed=64 * pairs // LANES, transcendentals=pairs)
 
-    boxes = gather_near(send, short, long)
+    boxes = gather_near(send, short, long).reshape(count * ROWS, LANES)
     send, own, mid = pl.pallas_call(
         functools.partial(middle_kernel, sizes),
-        out_shape=(many, block, block),
+        out_shape=(jax.ShapeDtypeStruct((6 * copies, LANES), jnp.float32), block, block),
         in_specs=[vmem] * 6,
         out_specs=(vmem,) * 3,
         scratch_shapes=scratch,
@@ -335,18 +350,18 @@
         cost_estimate=cost,
         name="middle",
     )(boxes, own, mid, mass, charge, label)
-    boxes = gather_near(send, short, long)
+    places = gather_near(send.reshape(copies, 1, 6 * LANES), short, long)
     whole = jax.ShapeDtypeStruct(positions.shape, jnp.float32)
     return pl.pallas_call(
         functools.partial(last_kernel, sizes),
         out_shape=(whole, whole, whole),
-        in_specs=[vmem] * 6,
+        in_specs=[vmem] * 7,
         out_specs=(vmem,) * 3,
         scratch_shapes=scratch,
         compiler_params=small,
         cost_estimate=cost,
         name="last",
-    )(boxes, own, mid, mass, charge, label)
+    )(boxes, places.reshape(6 * count, LANES), own, mid, mass, charge, label)
 
 
 def solution(mesh):

time: 40.4 us -> 40.1 us (level); the launches traced: 40.2 us -> 40.8 us
  Pallas kernels: 14.2 us -> 15 us
    pallas_call x1, Pallas kernels: 6.96 us -> 7.36 us  [local(): pl.pallas_call(functools.partial(last_kernel, sizes), out_shape=(whole, w...]
where the time goes in v5:
time: 40.1 us; the launch traced here: 40.8 us
  blocking collectives  24.6 us (61%)
  Pallas kernels  15 us (37%)
  between operations  1.3 us (3%)
    all_to_all x2, blocking collectives, gather_near(): boxes = lax.all_to_all(copies, short, 0, 0, tiled=True)  24.6 us
    pallas_call x1, Pallas kernels, local(): pl.pallas_call(functools.partial(last_kernel, sizes), out_shape=(whole, w...  7.36 us
    pallas_call x1, Pallas kernels, local(): pl.pallas_call(functools.partial(middle_kernel, sizes), out_shape=(jax.Sh...  6.76 us
    pallas_call x1, Pallas kernels, local(): pl.pallas_call(start_kernel, out_shape=(many, block, block, block, block,...  0.84 us

profile of v5, /device:TPU:0, one launch (start us, length us, event | category | flops | bytes accessed | tf_op | source)
XLA Modules:
  0.0 40.8 jit_solution(2037393225158896994)
XLA Ops:
  1.3 0.8 %start.1 = (f32[32,8,128]{2,1,0:T(8,128)S(1)}, f32[8,128]{1,0:T(8,128)S(1)}, f32[8,128]{1,0:T(8,128)S(1)}, f32[8,128]{1,0:T(8,128)S(1)}, f32[8,128]{1,0:T(8,128)S(1)}, /*index=5*/s32[1,1,1,256]{3,2,1,0:T(1,128)S(1)}) custom-call(f32[3,1,1,1,256]{4,3,2,1,0:T(1,128)} %pos.1, f32[3,1,1,1,256]{4,3,2,1,0:T(1,128)} %vel.1, f32[3,1,1,1,256]{4,3,2,1,0:T(1,128)} %frc.1, ...), custom_call_target="tpu_custom_call" | custom-call | tf_op jit(solution)/shard_map/start/pallas_call | solution.py:317
  2.1 14.9 %all_to_all.10 = f32[32,8,128]{2,1,0:T(8,128)S(1)} all-to-all(f32[32,8,128]{2,1,0:T(8,128)S(1)} %get-tuple-element.12), channel_id=1, replica_groups=mesh['gx'=4,'gy'=2,'gz'=4] {'gx','gy','gz'}, dimensions={0} | all-to-all | bytes 262144 | tf_op jit(solution)/shard_map/all_to_all | solution.py:294
  17.1 6.8 %middle.1 = (f32[192,128]{1,0:T(8,128)S(1)}, f32[8,128]{1,0:T(8,128)S(1)}, f32[8,128]{1,0:T(8,128)S(1)}) custom-call(f32[256,128]{1,0:T(8,128)S(1)} %bitcast.3, f32[8,128]{1,0:T(8,128)S(1)} %get-tuple-element.13.own, f32[8,128]{1,0:T(8,128)S(1)} %get-tuple-element.14.mid, f32[8,128]{1,0:T(8,128)S(1)} %get-tuple-element.15.mass, ...), custom_call_target="tpu_custom_call" | custom-call | flops 54525952 | bytes 1048576 | tf_op jit(solution)/shard_map/middle/pallas_call | solution.py:343
  23.8 9.6 %all_to_all.11 = f32[32,1,768]{2,1,0:T(1,128)S(1)} all-to-all(f32[32,1,768]{2,1,0:T(1,128)S(1)} %bitcast.6), channel_id=1, replica_groups=mesh['gx'=4,'gy'=2,'gz'=4] {'gx','gy','gz'}, dimensions={0} | all-to-all | bytes 196608 | tf_op jit(solution)/shard_map/all_to_all | solution.py:294
  33.5 7.4 %last.1 = (f32[3,1,1,1,256]{4,3,2,1,0:T(1,128)}, f32[3,1,1,1,256]{4,3,2,1,0:T(1,128)}, f32[3,1,1,1,256]{4,3,2,1,0:T(1,128)}) custom-call(f32[256,128]{1,0:T(8,128)S(1)} %bitcast.4, f32[192,128]{1,0:T(8,128)S(1)} %bitcast.5, f32[8,128]{1,0:T(8,128)S(1)} %get-tuple-element.19.own, f32[8,128]{1,0:T(8,128)S(1)} %get-tuple-element.20.mid, ...), custom_call_target="tpu_custom_call" | custom-call | flops 54525952 | bytes 1048576 | tf_op jit(solution)/shard_map/last/pallas_call | solution.py:355

commit v6 on v5

--- a/solution.py
+++ b/solution.py
@@ -69,7 +69,7 @@
     switch = jnp.maximum(jnp.float32(sizes.top) - squared, 0.0)
     root = lax.rsqrt(squared + jnp.float32(sizes.soft))
     first = switch * root
-    return parts, (first * first) * (root * charge)
+    return parts, (first * root) * (first * charge)
 
 
 def start_kernel(pos, vel, frc, chg, imass, lab, occ, send, own, mid, mass, charge, label,
@@ -107,16 +107,10 @@
         send[b] = block
 
 
-def prepare(own, charge, labels, targets, sizes):
+def prepare(own, charge, labels, sizes):
     mine = to_steps(own[...], row_constant([1.0 / length for length in sizes.lengths]))
     aim = mine + seam_shift(own[...], sizes)
     columns = jnp.transpose(aim)
-    for c in range(3):
-        for h in range(2):
-            for g in range(LANES // ROWS):
-                column = columns[ROWS * g : ROWS * g + ROWS, 2 * c + h : 2 * c + h + 1]
-                spot = h * (LANES // ROWS) + g
-                targets[c, spot] = jnp.broadcast_to(column, (ROWS, LANES))
 
     def spread(array):
         line = jnp.concatenate([array[0:1, :], array[1:2, :]], axis=1)
@@ -134,21 +128,34 @@
     other = slot + 3 - away
     same = (shifted(label) == label) & (other >= 0) & (other < 2 * LANES) & (away < 7)
     parts, base = pair_weight(here, there, jnp.where(same, charge_there, 0.0), sizes)
-    return [jnp.sum(base * parts[c], axis=0, keepdims=True) for c in range(3)]
-
-
-def add_tiles(tiles, targets, sums, sizes):
+    return columns, [jnp.sum(base * parts[c], axis=0, keepdims=True) for c in range(3)]
+
+
+def add_tiles(tiles, columns, targets, sums, sizes):
     for g in range(2 * LANES // ROWS):
-        target = [targets[c, g] for c in range(3)]
+        if columns is None:
+            target = [targets[c, g] for c in range(3)]
+        else:
+            half, spot = divmod(g * ROWS, LANES)
+            target = [
+                jnp.broadcast_to(
+                    columns[spot : spot + ROWS, 2 * c + half : 2 * c + half + 1], (ROWS, LANES)
+                )
+                for c in range(3)
+            ]
+            for c in range(3):
+                targets[c, g] = target[c]
         added = [None] * 3
         for source, charge in tiles:
             parts, base = pair_weight(target, source, charge, sizes)
             for c in range(3):
                 product = base * parts[c]
+                if added[c] is None and columns is None:
+                    added[c] = sums[c, ROWS * g : ROWS * g + ROWS, :]
                 added[c] = product if added[c] is None else added[c] + product
         for c in range(3):
             rows = slice(ROWS * g, ROWS * g + ROWS)
-            sums[c, rows, :] = sums[c, rows, :] + added[c]
+            sums[c, rows, :] = added[c]
 
 
 def force_of(charges, places, per, own, charge, labels, steps, packed, packed_charges, offsets,
@@ -156,9 +163,7 @@
     count = charges.shape[0] // ROWS
     stride = 2 if count % 2 == 0 else 1
     lane = lax.broadcasted_iota(jnp.int32, (ROWS, LANES), 1)
-    within = prepare(own, charge, labels, targets, sizes)
-    for c in range(3):
-        sums[c] = jnp.zeros(sums.shape[1:], jnp.float32)
+    columns, within = prepare(own, charge, labels, sizes)
 
     inverses = {}
     for k in range(pl.cdiv(places.shape[0], ROWS)):
@@ -176,13 +181,13 @@
     def one(ref, row):
         return jnp.broadcast_to(ref[pl.ds(row, 1), :], (ROWS, LANES))
 
-    def heads(k, unused):
+    def heads(k, unused, fresh=None):
         boxes = [k * stride + u for u in range(stride)]
         tiles = [
             ([one(steps, b * per + 2 * c) for c in range(3)], one(charges, b * ROWS + 6))
             for b in boxes
         ]
-        add_tiles(tiles, targets, sums, sizes)
+        add_tiles(tiles, fresh, targets, sums, sizes)
         for b in boxes:
             position = offsets[b]
             tile = position // LANES
@@ -205,7 +210,8 @@
     for b in range(count):
         offsets[b] = position
         position = position + filled[b, 0]
-    lax.fori_loop(0, count // stride, heads, 0)
+    heads(0, 0, columns)
+    lax.fori_loop(1, count // stride, heads, 0)
     filled_tiles = (position + (LANES - 1)) // LANES
     for u in range(stride):
         packed_charges[filled_tiles + u] = jnp.zeros((ROWS, LANES), jnp.float32)
@@ -221,7 +227,7 @@
             )
             for t in [k * stride + u for u in range(stride)]
         ]
-        add_tiles(tiles, targets, sums, sizes)
+        add_tiles(tiles, None, targets, sums, sizes)
         return unused
 
     lax.fori_loop(0, (filled_tiles + stride - 1) // stride, tails, 0)

time: 40.1 us -> 40.2 us (level); the launches traced: 40.8 us -> 40 us
  Pallas kernels: 15 us -> 14.1 us
    pallas_call x1, Pallas kernels: 7.36 us -> 6.93 us  [local(): pl.pallas_call(functools.partial(last_kernel, sizes), out_shape=(whole, w...]
where the time goes in v6:
time: 40.2 us; the launch traced here: 40 us
  blocking collectives  24.6 us (61%)
  Pallas kernels  14.1 us (35%)
  between operations  1.3 us (3%)
    all_to_all x2, blocking collectives, gather_near(): boxes = lax.all_to_all(copies, short, 0, 0, tiled=True)  24.6 us
    pallas_call x1, Pallas kernels, local(): pl.pallas_call(functools.partial(last_kernel, sizes), out_shape=(whole, w...  6.93 us
    pallas_call x1, Pallas kernels, local(): pl.pallas_call(functools.partial(middle_kernel, sizes), out_shape=(jax.Sh...  6.36 us
    pallas_call x1, Pallas kernels, local(): pl.pallas_call(start_kernel, out_shape=(many, block, block, block, block,...  0.84 us

profile of v6, /device:TPU:0, one launch (start us, length us, event | category | flops | bytes accessed | tf_op | source)
XLA Modules:
  0.0 40.0 jit_solution(1551249515482108313)
XLA Ops:
  1.3 0.8 %start.1 = (f32[32,8,128]{2,1,0:T(8,128)S(1)}, f32[8,128]{1,0:T(8,128)S(1)}, f32[8,128]{1,0:T(8,128)S(1)}, f32[8,128]{1,0:T(8,128)S(1)}, f32[8,128]{1,0:T(8,128)S(1)}, /*index=5*/s32[1,1,1,256]{3,2,1,0:T(1,128)S(1)}) custom-call(f32[3,1,1,1,256]{4,3,2,1,0:T(1,128)} %pos.1, f32[3,1,1,1,256]{4,3,2,1,0:T(1,128)} %vel.1, f32[3,1,1,1,256]{4,3,2,1,0:T(1,128)} %frc.1, ...), custom_call_target="tpu_custom_call" | custom-call | tf_op jit(solution)/shard_map/start/pallas_call | solution.py:323
  2.1 14.9 %all_to_all.10 = f32[32,8,128]{2,1,0:T(8,128)S(1)} all-to-all(f32[32,8,128]{2,1,0:T(8,128)S(1)} %get-tuple-element.12), channel_id=1, replica_groups=mesh['gx'=4,'gy'=2,'gz'=4] {'gx','gy','gz'}, dimensions={0} | all-to-all | bytes 262144 | tf_op jit(solution)/shard_map/all_to_all | solution.py:300
  17.1 6.4 %middle.1 = (f32[192,128]{1,0:T(8,128)S(1)}, f32[8,128]{1,0:T(8,128)S(1)}, f32[8,128]{1,0:T(8,128)S(1)}) custom-call(f32[256,128]{1,0:T(8,128)S(1)} %bitcast.3, f32[8,128]{1,0:T(8,128)S(1)} %get-tuple-element.13.own, f32[8,128]{1,0:T(8,128)S(1)} %get-tuple-element.14.mid, f32[8,128]{1,0:T(8,128)S(1)} %get-tuple-element.15.mass, ...), custom_call_target="tpu_custom_call" | custom-call | flops 54525952 | bytes 1048576 | tf_op jit(solution)/shard_map/middle/pallas_call | solution.py:349
  23.4 9.6 %all_to_all.11 = f32[32,1,768]{2,1,0:T(1,128)S(1)} all-to-all(f32[32,1,768]{2,1,0:T(1,128)S(1)} %bitcast.6), channel_id=1, replica_groups=mesh['gx'=4,'gy'=2,'gz'=4] {'gx','gy','gz'}, dimensions={0} | all-to-all | bytes 196608 | tf_op jit(solution)/shard_map/all_to_all | solution.py:300
  33.1 6.9 %last.1 = (f32[3,1,1,1,256]{4,3,2,1,0:T(1,128)}, f32[3,1,1,1,256]{4,3,2,1,0:T(1,128)}, f32[3,1,1,1,256]{4,3,2,1,0:T(1,128)}) custom-call(f32[256,128]{1,0:T(8,128)S(1)} %bitcast.4, f32[192,128]{1,0:T(8,128)S(1)} %bitcast.5, f32[8,128]{1,0:T(8,128)S(1)} %get-tuple-element.19.own, f32[8,128]{1,0:T(8,128)S(1)} %get-tuple-element.20.mid, ...), custom_call_target="tpu_custom_call" | custom-call | flops 54525952 | bytes 1048576 | tf_op jit(solution)/shard_map/last/pallas_call | solution.py:361

commit v7 on v6

--- a/solution.py
+++ b/solution.py
@@ -13,14 +13,14 @@
 time_step = 0.1
 half_step = 0.05
 
-LANES = 128
 ROWS = 8
 TIES = (128, 191)
 FULL = 4294967296.0
 
 
 class Sizes:
-    def __init__(self, lengths):
+    def __init__(self, lengths, slots):
+        self.half = slots // 2
         self.lengths = lengths
         self.unit = max(set(lengths), key=lengths.count)
         step = self.unit / FULL
@@ -33,9 +33,9 @@
         self.seam = [length * length / 4 < cutoff_square for length in lengths]
 
 
-def row_constant(values):
-    row = lax.broadcasted_iota(jnp.int32, (ROWS, LANES), 0) // 2
-    out = jnp.zeros((ROWS, LANES), jnp.float32)
+def row_constant(values, half):
+    row = lax.broadcasted_iota(jnp.int32, (ROWS, half), 0) // 2
+    out = jnp.zeros((ROWS, half), jnp.float32)
     for c, value in enumerate(values):
         out = jnp.where(row == c, jnp.float32(value), out)
     return out
@@ -49,8 +49,8 @@
 
 
 def seam_shift(places, sizes):
-    row = lax.broadcasted_iota(jnp.int32, (ROWS, LANES), 0) // 2
-    shift = jnp.zeros((ROWS, LANES), jnp.int32)
+    row = lax.broadcasted_iota(jnp.int32, (ROWS, sizes.half), 0) // 2
+    shift = jnp.zeros((ROWS, sizes.half), jnp.int32)
     for c, length in enumerate(sizes.lengths):
         if sizes.seam[c]:
             near = jnp.where(jnp.abs(places) < length / 4, TIES[0], TIES[1])
@@ -72,7 +72,7 @@
     return parts, (first * root) * (first * charge)
 
 
-def start_kernel(pos, vel, frc, chg, imass, lab, occ, send, own, mid, mass, charge, label,
+def start_kernel(sizes, pos, vel, frc, chg, imass, lab, occ, send, own, mid, mass, charge, label,
                  pos_in, vel_in, frc_in, chg_in, imass_in, sems):
     copies = [
         pltpu.make_async_copy(source, target, sems.at[i])
@@ -84,11 +84,11 @@
         copy.start()
     for copy in copies:
         copy.wait()
-    live = lax.broadcasted_iota(jnp.int32, (1, 2 * LANES), 1) < occ[0, 0, 0]
+    live = lax.broadcasted_iota(jnp.int32, (1, 2 * sizes.half), 1) < occ[0, 0, 0]
     live_charge = jnp.where(live, chg_in[0, 0], 0.0)
     inverse = imass_in[0, 0]
     for h in range(2):
-        cut = slice(h * LANES, (h + 1) * LANES)
+        cut = slice(h * sizes.half, (h + 1) * sizes.half)
         for c in range(3):
             r = slice(2 * c + h, 2 * c + h + 1)
             midway = vel_in[c, 0, 0] + half_step * inverse * frc_in[c, 0, 0]
@@ -99,47 +99,47 @@
             charge[r, :] = live_charge[:, cut]
         r = slice(6 + h, 7 + h)
         own[r, :] = live_charge[:, cut]
-        mid[r, :] = jnp.zeros((1, LANES), jnp.float32)
-        mass[r, :] = jnp.zeros((1, LANES), jnp.float32)
-        charge[r, :] = jnp.zeros((1, LANES), jnp.float32)
+        mid[r, :] = jnp.zeros((1, sizes.half), jnp.float32)
+        mass[r, :] = jnp.zeros((1, sizes.half), jnp.float32)
+        charge[r, :] = jnp.zeros((1, sizes.half), jnp.float32)
     block = own[...]
     for b in range(send.shape[0]):
         send[b] = block
 
 
 def prepare(own, charge, labels, sizes):
-    mine = to_steps(own[...], row_constant([1.0 / length for length in sizes.lengths]))
+    mine = to_steps(own[...], row_constant([1.0 / length for length in sizes.lengths], sizes.half))
     aim = mine + seam_shift(own[...], sizes)
     columns = jnp.transpose(aim)
 
     def spread(array):
         line = jnp.concatenate([array[0:1, :], array[1:2, :]], axis=1)
-        return jnp.broadcast_to(line, (ROWS, 2 * LANES))
+        return jnp.broadcast_to(line, (ROWS, 2 * sizes.half))
 
     def shifted(array):
-        return pltpu.roll(pltpu.roll(array, 2 * LANES - 3, 1), 0, 1, stride=1, stride_axis=0)
+        return pltpu.roll(pltpu.roll(array, 2 * sizes.half - 3, 1), 0, 1, stride=1, stride_axis=0)
 
     here = [spread(aim[2 * c : 2 * c + 2]) for c in range(3)]
     there = [shifted(spread(mine[2 * c : 2 * c + 2])) for c in range(3)]
     charge_there = shifted(spread(charge[0:2, :]))
-    label = jnp.broadcast_to(labels[0, 0], (ROWS, 2 * LANES))
-    slot = lax.broadcasted_iota(jnp.int32, (ROWS, 2 * LANES), 1)
-    away = lax.broadcasted_iota(jnp.int32, (ROWS, 2 * LANES), 0)
+    label = jnp.broadcast_to(labels[0, 0], (ROWS, 2 * sizes.half))
+    slot = lax.broadcasted_iota(jnp.int32, (ROWS, 2 * sizes.half), 1)
+    away = lax.broadcasted_iota(jnp.int32, (ROWS, 2 * sizes.half), 0)
     other = slot + 3 - away
-    same = (shifted(label) == label) & (other >= 0) & (other < 2 * LANES) & (away < 7)
+    same = (shifted(label) == label) & (other >= 0) & (other < 2 * sizes.half) & (away < 7)
     parts, base = pair_weight(here, there, jnp.where(same, charge_there, 0.0), sizes)
     return columns, [jnp.sum(base * parts[c], axis=0, keepdims=True) for c in range(3)]
 
 
 def add_tiles(tiles, columns, targets, sums, sizes):
-    for g in range(2 * LANES // ROWS):
+    for g in range(2 * sizes.half // ROWS):
         if columns is None:
             target = [targets[c, g] for c in range(3)]
         else:
-            half, spot = divmod(g * ROWS, LANES)
+            half, spot = divmod(g * ROWS, sizes.half)
             target = [
                 jnp.broadcast_to(
-                    columns[spot : spot + ROWS, 2 * c + half : 2 * c + half + 1], (ROWS, LANES)
+                    columns[spot : spot + ROWS, 2 * c + half : 2 * c + half + 1], (ROWS, sizes.half)
                 )
                 for c in range(3)
             ]
@@ -162,15 +162,15 @@
              targets, sums, sizes):
     count = charges.shape[0] // ROWS
     stride = 2 if count % 2 == 0 else 1
-    lane = lax.broadcasted_iota(jnp.int32, (ROWS, LANES), 1)
+    lane = lax.broadcasted_iota(jnp.int32, (ROWS, sizes.half), 1)
     columns, within = prepare(own, charge, labels, sizes)
 
     inverses = {}
     for k in range(pl.cdiv(places.shape[0], ROWS)):
         begin = (ROWS * k) % per
         if begin not in inverses:
-            axis = lax.rem(lax.broadcasted_iota(jnp.int32, (ROWS, LANES), 0) + begin, per) // 2
-            inverse = jnp.zeros((ROWS, LANES), jnp.float32)
+            axis = lax.rem(lax.broadcasted_iota(jnp.int32, (ROWS, sizes.half), 0) + begin, per) // 2
+            inverse = jnp.zeros((ROWS, sizes.half), jnp.float32)
             for c, length in enumerate(sizes.lengths):
                 inverse = jnp.where(axis == c, jnp.float32(1.0 / length), inverse)
             inverses[begin] = inverse
@@ -179,7 +179,7 @@
         steps[rows, :] = to_steps(places[rows, :], inverses[begin][:size])
 
     def one(ref, row):
-        return jnp.broadcast_to(ref[pl.ds(row, 1), :], (ROWS, LANES))
+        return jnp.broadcast_to(ref[pl.ds(row, 1), :], (ROWS, sizes.half))
 
     def heads(k, unused, fresh=None):
         boxes = [k * stride + u for u in range(stride)]
@@ -190,8 +190,8 @@
         add_tiles(tiles, fresh, targets, sums, sizes)
         for b in boxes:
             position = offsets[b]
-            tile = position // LANES
-            begin = lax.rem(position, LANES)
+            tile = position // sizes.half
+            begin = lax.rem(position, sizes.half)
             late = lane >= begin
             moved = pltpu.roll(steps[pl.ds(b * per, ROWS), :], begin, 1)
             pltpu.store(packed.at[tile], moved, mask=late)
@@ -212,18 +212,18 @@
         position = position + filled[b, 0]
     heads(0, 0, columns)
     lax.fori_loop(1, count // stride, heads, 0)
-    filled_tiles = (position + (LANES - 1)) // LANES
+    filled_tiles = (position + (sizes.half - 1)) // sizes.half
     for u in range(stride):
-        packed_charges[filled_tiles + u] = jnp.zeros((ROWS, LANES), jnp.float32)
+        packed_charges[filled_tiles + u] = jnp.zeros((ROWS, sizes.half), jnp.float32)
 
     def tails(k, unused):
         tiles = [
             (
                 [
-                    jnp.broadcast_to(packed[t, 2 * c + 1 : 2 * c + 2, :], (ROWS, LANES))
+                    jnp.broadcast_to(packed[t, 2 * c + 1 : 2 * c + 2, :], (ROWS, sizes.half))
                     for c in range(3)
                 ],
-                jnp.broadcast_to(packed_charges[t, 7:8, :], (ROWS, LANES)),
+                jnp.broadcast_to(packed_charges[t, 7:8, :], (ROWS, sizes.half)),
             )
             for t in [k * stride + u for u in range(stride)]
         ]
@@ -232,12 +232,12 @@
 
     lax.fori_loop(0, (filled_tiles + stride - 1) // stride, tails, 0)
 
-    row = lax.broadcasted_iota(jnp.int32, (ROWS, LANES), 0)
-    ones = jnp.ones((ROWS, LANES), jnp.bfloat16)
-    result = jnp.zeros((ROWS, LANES), jnp.float32)
+    row = lax.broadcasted_iota(jnp.int32, (ROWS, sizes.half), 0)
+    ones = jnp.ones((ROWS, sizes.half), jnp.bfloat16)
+    result = jnp.zeros((ROWS, sizes.half), jnp.float32)
     for c in range(3):
         left = sums[c]
-        total = jnp.zeros((ROWS, 2 * LANES), jnp.float32)
+        total = jnp.zeros((ROWS, 2 * sizes.half), jnp.float32)
         for piece in range(3):
             part = left.astype(jnp.bfloat16)
             left = left - part.astype(jnp.float32)
@@ -246,7 +246,7 @@
             )
         total = (total - within[c]) * jnp.float32(sizes.scale[c])
         for h in range(2):
-            result = jnp.where(row == 2 * c + h, total[:, h * LANES : (h + 1) * LANES], result)
+            result = jnp.where(row == 2 * c + h, total[:, h * sizes.half : (h + 1) * sizes.half], result)
     return charge[...] * result
 
 
@@ -255,7 +255,7 @@
     kick = half_step * mass[...] * force
     midway = (mid[...] + kick) + kick
     places = own[...] + time_step * midway
-    row = lax.broadcasted_iota(jnp.int32, (ROWS, LANES), 0)
+    row = lax.broadcasted_iota(jnp.int32, (ROWS, sizes.half), 0)
     block = jnp.where(row < 6, places, own[...])
     own_out[...] = block
     mid_out[...] = midway
@@ -276,7 +276,7 @@
     for c in range(3):
         for h in range(2):
             r = slice(2 * c + h, 2 * c + h + 1)
-            cut = slice(h * LANES, (h + 1) * LANES)
+            cut = slice(h * sizes.half, (h + 1) * sizes.half)
             pos[c, 0, 0, :, cut] = places[r, :]
             vel[c, 0, 0, :, cut] = velocity[r, :]
             frc[c, 0, 0, :, cut] = force[r, :]
@@ -309,7 +309,7 @@
 def local(positions, velocities, forces, charges, inverse_mass, occupancy, molecule):
     axes = ("gx", "gy", "gz")
     extents = [lax.axis_size(axis) for axis in axes]
-    sizes = Sizes([float(extent) for extent in extents])
+    sizes = Sizes([float(extent) for extent in extents], positions.shape[-1])
     short = tuple(axis for axis, extent in zip(axes, extents) if extent < 5)
     long = tuple(axis for axis, extent in zip(axes, extents) if extent >= 5)
     copies = math.prod([1] + [extent for extent in extents if extent < 5])
@@ -318,10 +318,10 @@
     vmem = pl.BlockSpec(memory_space=pltpu.VMEM)
     smem = pl.BlockSpec(memory_space=pltpu.SMEM)
     small = pltpu.CompilerParams(vmem_limit_bytes=8 * 1024 * 1024)
-    block = jax.ShapeDtypeStruct((ROWS, LANES), jnp.float32)
-    many = jax.ShapeDtypeStruct((copies, ROWS, LANES), jnp.float32)
+    block = jax.ShapeDtypeStruct((ROWS, sizes.half), jnp.float32)
+    many = jax.ShapeDtypeStruct((copies, ROWS, sizes.half), jnp.float32)
     send, own, mid, mass, charge, label = pl.pallas_call(
-        start_kernel,
+        functools.partial(start_kernel, sizes),
         out_shape=(many, block, block, block, block, jax.ShapeDtypeStruct(molecule.shape, jnp.int32)),
         in_specs=[pl.BlockSpec(memory_space=pltpu.HBM)] * 6 + [smem],
         out_specs=(vmem,) * 6,
@@ -334,21 +334,21 @@
         name="start",
     )(*[pltpu.with_memory_space_constraint(array, pltpu.HBM) for array in (positions, velocities, forces, charges, inverse_mass, molecule)], occupancy)
 
-    pairs = 2 * LANES * LANES * 2 * count
+    pairs = 2 * sizes.half * sizes.half * 2 * count
     scratch = [
-        pltpu.VMEM((ROWS * (count + 1), LANES), jnp.int32),
-        pltpu.VMEM((count + 4, ROWS, LANES), jnp.int32),
-        pltpu.VMEM((count + 4, ROWS, LANES), jnp.float32),
+        pltpu.VMEM((ROWS * (count + 1), sizes.half), jnp.int32),
+        pltpu.VMEM((count + 4, ROWS, sizes.half), jnp.int32),
+        pltpu.VMEM((count + 4, ROWS, sizes.half), jnp.float32),
         pltpu.SMEM((count,), jnp.int32),
-        pltpu.VMEM((3, 2 * LANES // ROWS, ROWS, LANES), jnp.int32),
-        pltpu.VMEM((3, 2 * LANES, LANES), jnp.float32),
+        pltpu.VMEM((3, 2 * sizes.half // ROWS, ROWS, sizes.half), jnp.int32),
+        pltpu.VMEM((3, 2 * sizes.half, sizes.half), jnp.float32),
     ]
-    cost = pl.CostEstimate(flops=26 * pairs, bytes_accessed=64 * pairs // LANES, transcendentals=pairs)
-
-    boxes = gather_near(send, short, long).reshape(count * ROWS, LANES)
+    cost = pl.CostEstimate(flops=26 * pairs, bytes_accessed=64 * pairs // sizes.half, transcendentals=pairs)
+
+    boxes = gather_near(send, short, long).reshape(count * ROWS, sizes.half)
     send, own, mid = pl.pallas_call(
         functools.partial(middle_kernel, sizes),
-        out_shape=(jax.ShapeDtypeStruct((6 * copies, LANES), jnp.float32), block, block),
+        out_shape=(jax.ShapeDtypeStruct((6 * copies, sizes.half), jnp.float32), block, block),
         in_specs=[vmem] * 6,
         out_specs=(vmem,) * 3,
         scratch_shapes=scratch,
@@ -356,7 +356,7 @@
         cost_estimate=cost,
         name="middle",
     )(boxes, own, mid, mass, charge, label)
-    places = gather_near(send.reshape(copies, 1, 6 * LANES), short, long)
+    places = gather_near(send.reshape(copies, 1, 6 * sizes.half), short, long)
     whole = jax.ShapeDtypeStruct(positions.shape, jnp.float32)
     return pl.pallas_call(
         functools.partial(last_kernel, sizes),
@@ -367,7 +367,7 @@
         compiler_params=small,
         cost_estimate=cost,
         name="last",
-    )(boxes, places.reshape(6 * count, LANES), own, mid, mass, charge, label)
+    )(boxes, places.reshape(6 * count, sizes.half), own, mid, mass, charge, label)
 
 
 def solution(mesh):

time: 40.2 us -> 39.7 us (0.988)
  no operation moved by 1% of the time
where the time goes in v7:
time: 39.7 us; the launch traced here: 39.5 us
  blocking collectives  24.6 us (62%)
  Pallas kernels  13.7 us (35%)
  between operations  1.3 us (3%)
    all_to_all x2, blocking collectives, gather_near(): boxes = lax.all_to_all(copies, short, 0, 0, tiled=True)  24.6 us
    pallas_call x1, Pallas kernels, local(): pl.pallas_call(functools.partial(last_kernel, sizes), out_shape=(whole, w...  6.7 us
    pallas_call x1, Pallas kernels, local(): pl.pallas_call(functools.partial(middle_kernel, sizes), out_shape=(jax.Sh...  6.12 us
    pallas_call x1, Pallas kernels, local(): pl.pallas_call(functools.partial(start_kernel, sizes), out_shape=(many, b...  0.84 us

profile of v7, /device:TPU:0, one launch (start us, length us, event | category | flops | bytes accessed | tf_op | source)
XLA Modules:
  0.0 39.5 jit_solution(1551249515482108313)
XLA Ops:
  1.3 0.8 %start.1 = (f32[32,8,128]{2,1,0:T(8,128)S(1)}, f32[8,128]{1,0:T(8,128)S(1)}, f32[8,128]{1,0:T(8,128)S(1)}, f32[8,128]{1,0:T(8,128)S(1)}, f32[8,128]{1,0:T(8,128)S(1)}, /*index=5*/s32[1,1,1,256]{3,2,1,0:T(1,128)S(1)}) custom-call(f32[3,1,1,1,256]{4,3,2,1,0:T(1,128)} %pos.1, f32[3,1,1,1,256]{4,3,2,1,0:T(1,128)} %vel.1, f32[3,1,1,1,256]{4,3,2,1,0:T(1,128)} %frc.1, ...), custom_call_target="tpu_custom_call" | custom-call | tf_op jit(solution)/shard_map/start/pallas_call | solution.py:323
  2.1 14.9 %all_to_all.10 = f32[32,8,128]{2,1,0:T(8,128)S(1)} all-to-all(f32[32,8,128]{2,1,0:T(8,128)S(1)} %get-tuple-element.12), channel_id=1, replica_groups=mesh['gx'=4,'gy'=2,'gz'=4] {'gx','gy','gz'}, dimensions={0} | all-to-all | bytes 262144 | tf_op jit(solution)/shard_map/all_to_all | solution.py:300
  17.1 6.1 %middle.1 = (f32[192,128]{1,0:T(8,128)S(1)}, f32[8,128]{1,0:T(8,128)S(1)}, f32[8,128]{1,0:T(8,128)S(1)}) custom-call(f32[256,128]{1,0:T(8,128)S(1)} %bitcast.3, f32[8,128]{1,0:T(8,128)S(1)} %get-tuple-element.13.own, f32[8,128]{1,0:T(8,128)S(1)} %get-tuple-element.14.mid, f32[8,128]{1,0:T(8,128)S(1)} %get-tuple-element.15.mass, ...), custom_call_target="tpu_custom_call" | custom-call | flops 54525952 | bytes 1048576 | tf_op jit(solution)/shard_map/middle/pallas_call | solution.py:349
  23.2 9.6 %all_to_all.11 = f32[32,1,768]{2,1,0:T(1,128)S(1)} all-to-all(f32[32,1,768]{2,1,0:T(1,128)S(1)} %bitcast.6), channel_id=1, replica_groups=mesh['gx'=4,'gy'=2,'gz'=4] {'gx','gy','gz'}, dimensions={0} | all-to-all | bytes 196608 | tf_op jit(solution)/shard_map/all_to_all | solution.py:300
  32.8 6.7 %last.1 = (f32[3,1,1,1,256]{4,3,2,1,0:T(1,128)}, f32[3,1,1,1,256]{4,3,2,1,0:T(1,128)}, f32[3,1,1,1,256]{4,3,2,1,0:T(1,128)}) custom-call(f32[256,128]{1,0:T(8,128)S(1)} %bitcast.4, f32[192,128]{1,0:T(8,128)S(1)} %bitcast.5, f32[8,128]{1,0:T(8,128)S(1)} %get-tuple-element.19.own, f32[8,128]{1,0:T(8,128)S(1)} %get-tuple-element.20.mid, ...), custom_call_target="tpu_custom_call" | custom-call | flops 54525952 | bytes 1048576 | tf_op jit(solution)/shard_map/last/pallas_call | solution.py:361
